TPU v7x, 128 devices: a whole 4x4x4 slice. The times are simulated.
128 devices in a mesh: rows: 4 (over z), cols: 8 (over y_hi, x), slabs: 4 (over y_lo, core).
Axes of the slice: x: 4, y: 4 (y_hi: 2, y_lo: 2; y = y_hi * 2 + y_lo), z: 4, core: 2. Of those that a mesh axis runs over, the one named last changes fastest.
Arguments:
- tracer: float32 [16, 512, 256, 128], P('rows', 'cols', 'slabs'), may hold values from 0.2 to 1.8
- crowding: float32 [16, 512, 256, 128], P('rows', 'cols', 'slabs'), may hold values from 0.5 to 2
Outputs:
- column_sum: float32 [16, 512, 256, 128], P('rows', 'cols', 'slabs')
- tracer_end: float32 [16, 512, 256, 128], P('rows', 'cols', 'slabs')
All inputs are finite; a program needn't handle non-finite values.
Results may differ from a plain program's by a relative error of at most 0.00002.
Values sent between devices are 32-bit elements; how exact they have to be, the bound alone decides.
No kernel may reach another device: no remote copies, remote signals or barrier semaphores. Data moves between devices by JAX's collectives and lax.ppermute only.
A program may use at most 320 MiB of HBM per device.

v0:
```python
import jax
import jax.numpy as jnp
from jax import lax
from jax.sharding import PartitionSpec as P

STEPS = 4


def extended(array, sides, width):
    edges = {}
    for axis, dim in sides:
        count, length = (lax.axis_size(axis), array.shape[dim])
        up = [(i, (i + 1) % count) for i in range(count - 1)]
        last = lax.slice_in_dim(array, length - width, length, axis=dim)
        initial = lax.slice_in_dim(array, 0, width, axis=dim)
        edges[dim] = (
            lax.ppermute(last, axis, up),
            lax.ppermute(initial, axis, [(b, a) for a, b in up]),
        )
    done = []
    for _, dim in sides:
        low, high = edges[dim]
        around = [(width, width) if d in done else (0, 0) for d in range(array.ndim)]
        array = jnp.concatenate([jnp.pad(low, around), array, jnp.pad(high, around)], axis=dim)
        done.append(dim)
    return array


def prefix(array, axis, combine, identity):
    count, place = (lax.axis_size(axis), lax.axis_index(axis))
    everything = lax.all_gather(array, axis)
    start = jnp.broadcast_to(jnp.asarray(identity, array.dtype), array.shape)

    def turn(k, before):
        reached = k < place
        new = combine(before, everything[k])
        return jnp.where(reached, new, before)

    return lax.fori_loop(0, count, turn, start)


def inner_cells(values, dims):
    for dim in dims:
        values = lax.slice_in_dim(values, 1, values.shape[dim] - 1, axis=dim)
    return values


def side_cells(values, dim, start, dims):
    others = [other for other in dims if other != dim]
    values = inner_cells(values, others)
    return lax.slice_in_dim(values, start, start + values.shape[dim] - 2, axis=dim)


def advance(padded, crowding):
    middle = inner_cells(padded, (0, 1, 2))
    lower = [side_cells(padded, dim, 0, (0, 1, 2)) for dim in (0, 1, 2)]
    upper = [side_cells(padded, dim, 2, (0, 1, 2)) for dim in (0, 1, 2)]
    spread = lower[0] + upper[0] + lower[1] + upper[1] + lower[2] + upper[2] - 6.0 * middle
    return middle + 0.1 * spread + 0.2 * middle * (1.0 - middle * crowding)


def body(tracer, crowding):
    for step in range(STEPS):
        padded = extended(tracer, (("rows", 0), ("cols", 1), ("slabs", 2)), 1)
        tracer = advance(padded, crowding)
    here = jnp.cumsum(tracer, axis=0)
    total = lax.slice_in_dim(here, here.shape[0] - 1, here.shape[0], axis=0)

    def add_pair(earlier_total, later_total):
        return earlier_total + later_total

    below = prefix(total, "rows", add_pair, jnp.zeros_like(total))
    column_sum = (here + below) / (tracer.shape[0] * lax.axis_size("rows"))
    return (column_sum, tracer)


def solution(mesh):
    placed = (P("rows", "cols", "slabs", None), P("rows", "cols", "slabs", None))
    return jax.shard_map(
        body,
        mesh=mesh,
        in_specs=placed,
        out_specs=(P("rows", "cols", "slabs", None), P("rows", "cols", "slabs", None)),
        check_vma=False,
    )
```

profile of v0, /device:TPU:1, one launch (start us, length us, event | category | flops | bytes accessed | tf_op | source)
XLA Modules:
  0.0 448.1 jit_solution(17947315886823089585)
XLA Ops:
  9.7 4.5 %collective-permute-start = (f32[1,64,64,128]{3,2,1,0:T(8,128)S(1)}, f32[1,64,64,128]{3,2,1,0:T(8,128)S(1)}, u32[]{:S(2)}, u32[]{:S(2)}) collective-permute-start(f32[1,64,64,128]{3,2,1,0:T(8,128)S(1)} %get-tuple-element.142), channel_id=1, source_target_pairs={{0,32},{32,64},{64,96},{1,33},{33,65},{65,97},{2,34},{34,66},{66,9... | collective-permute-start | bytes 6291464 | tf_op jit(solution)/shard_map/ppermute | solution.py:17
  16.5 3.1 collective-permute-start.2
  22.7 4.3 collective-permute-start.4
  29.0 29.4 %collective-permute-done = f32[1,64,64,128]{3,2,1,0:T(8,128)S(1)} collective-permute-done((f32[1,64,64,128]{3,2,1,0:T(8,128)S(1)}, f32[1,64,64,128]{3,2,1,0:T(8,128)S(1)}, u32[]{:S(2)}, u32[]{:S(2)}) %collective-permute-start) | collective-permute-done | bytes 2097184 | tf_op jit(solution)/shard_map/ppermute | solution.py:17
  60.0 8.9 %constant_dynamic-update-slice_fusion.1 = f32[6,64,64,128]{3,2,1,0:T(8,128)} fusion(f32[6,64,64,128]{3,2,1,0:T(8,128)} %constant_dynamic-update-slice_fusion.2, f32[4,64,64,128]{3,2,1,0:T(8,128)} %param.4), kind=kLoop, calls=%fused_computation.113 | loop fusion | bytes 16777216
  70.5 22.7 %fusion.38 = f32[4,64,64,128]{3,2,1,0:T(8,128)} fusion(f32[4,64,64,128]{3,2,1,0:T(8,128)} %param.4, f32[4,64,1,128]{3,2,1,0:T(1,128)S(1)} %bitcast.33, f32[6,1,64,128]{3,2,1,0:T(8,128)S(1)} %pad.51, f32[6,64,64,128]{3,2,1,0:T(8,128)} %constant_dynamic-update-slice_fusion, f32[6,1,64,128]{3,2,1,0:T(8,128)S(1)} %pad.50, f32[4,64,1,128]{3,2,1,0:T(1,128)S(1)} %bitcast.29, ...), kind=kLoop, calls=%fused_computation.94 | loop fusion | flops 62914560 | bytes 42598400 | tf_op jit(solution)/shard_map/add | solution.py:59
  95.7 4.2 collective-permute-start.6
  102.3 3.1 collective-permute-start.8
  108.5 5.2 %collective-permute-start.10 = (f32[4,64,1,128]{3,1,2,0:T(8,128)S(1)}, f32[4,64,1,128]{3,1,2,0:T(8,128)S(1)}, u32[]{:S(2)}, u32[]{:S(2)}) collective-permute-start(f32[4,64,1,128]{3,1,2,0:T(8,128)S(1)} %bitcast.43), channel_id=1, source_target_pairs={{0,1},{1,2},{2,3},{4,5},{5,6},{6,7},{8,9},{9,10},{10,11},{12,13},{... | collective-permute-start | bytes 393224 | tf_op jit(solution)/shard_map/ppermute | solution.py:17
  115.7 4.6 %collective-permute-done.11 = f32[4,64,1,128]{3,1,2,0:T(8,128)S(1)} collective-permute-done((f32[4,64,1,128]{3,1,2,0:T(8,128)S(1)}, f32[4,64,1,128]{3,1,2,0:T(8,128)S(1)}, u32[]{:S(2)}, u32[]{:S(2)}) %collective-permute-start.11) | collective-permute-done | bytes 131104 | tf_op jit(solution)/shard_map/ppermute | solution.py:18
  120.3 23.1 %collective-permute-done.6 = f32[1,64,64,128]{3,2,1,0:T(8,128)S(1)} collective-permute-done((f32[1,64,64,128]{3,2,1,0:T(8,128)S(1)}, f32[1,64,64,128]{3,2,1,0:T(8,128)S(1)}, u32[]{:S(2)}, u32[]{:S(2)}) %collective-permute-start.6) | collective-permute-done | bytes 2097184 | tf_op jit(solution)/shard_map/ppermute | solution.py:17
  143.3 4.1 collective-permute-done.7
  147.4 24.8 %fusion.27 = f32[4,64,64,128]{3,2,1,0:T(8,128)} fusion(f32[4,64,64,128]{3,2,1,0:T(8,128)} %fusion.38, f32[4,64,1,128]{3,2,1,0:T(1,128)S(1)} %bitcast.35, f32[6,1,64,128]{3,2,1,0:T(8,128)S(1)} %pad.55, f32[6,1,64,128]{3,2,1,0:T(8,128)S(1)} %pad.54, f32[1,64,64,128]{3,2,1,0:T(8,128)S(1)} %collective-permute-done.7, ...), kind=kLoop, calls=%fused_computation.65 | loop fusion | flops 79691776 | bytes 30015488 | tf_op jit(solution)/shard_map/add | solution.py:59
  174.7 3.4 collective-permute-start.12
  180.5 3.1 collective-permute-start.14
  186.7 6.3 %collective-permute-start.16 = (f32[4,64,1,128]{3,1,2,0:T(8,128)S(1)}, f32[4,64,1,128]{3,1,2,0:T(8,128)S(1)}, u32[]{:S(2)}, u32[]{:S(2)}) collective-permute-start(f32[4,64,1,128]{3,1,2,0:T(8,128)S(1)} %bitcast.44), channel_id=1, source_target_pairs={{0,1},{1,2},{2,3},{4,5},{5,6},{6,7},{8,9},{9,10},{10,11},{12,13},{... | collective-permute-start | bytes 393224 | tf_op jit(solution)/shard_map/ppermute | solution.py:17
  195.2 4.4 collective-permute-done.17
  199.6 20.8 %collective-permute-done.12 = f32[1,64,64,128]{3,2,1,0:T(8,128)S(1)} collective-permute-done((f32[1,64,64,128]{3,2,1,0:T(8,128)S(1)}, f32[1,64,64,128]{3,2,1,0:T(8,128)S(1)}, u32[]{:S(2)}, u32[]{:S(2)}) %collective-permute-start.12) | collective-permute-done | bytes 2097184 | tf_op jit(solution)/shard_map/ppermute | solution.py:17
  220.3 4.0 collective-permute-done.13
  224.3 24.6 %fusion.16 = f32[4,64,64,128]{3,2,1,0:T(8,128)} fusion(f32[4,64,64,128]{3,2,1,0:T(8,128)} %fusion.27, f32[4,64,1,128]{3,2,1,0:T(1,128)S(1)} %bitcast.36, f32[6,1,64,128]{3,2,1,0:T(8,128)S(1)} %pad.59, f32[6,1,64,128]{3,2,1,0:T(8,128)S(1)} %pad.58, f32[1,64,64,128]{3,2,1,0:T(8,128)S(1)} %collective-permute-done.13, ...), kind=kLoop, calls=%fused_computation.36 | loop fusion | flops 79691776 | bytes 30015488 | tf_op jit(solution)/shard_map/add | solution.py:59
  251.5 3.3 collective-permute-start.18
  257.0 3.1 collective-permute-start.20
  263.2 6.3 %collective-permute-start.23 = (f32[4,64,1,128]{3,1,2,0:T(8,128)S(1)}, f32[4,64,1,128]{3,1,2,0:T(8,128)S(1)}, u32[]{:S(2)}, u32[]{:S(2)}) collective-permute-start(f32[4,64,1,128]{3,1,2,0:T(8,128)S(1)} %bitcast.42), channel_id=1, source_target_pairs={{1,0},{2,1},{3,2},{5,4},{6,5},{7,6},{9,8},{10,9},{11,10},{13,12},{... | collective-permute-start | bytes 393224 | tf_op jit(solution)/shard_map/ppermute | solution.py:18
  269.5 3.1 collective-permute-start.22
  274.5 21.2 %collective-permute-done.18 = f32[1,64,64,128]{3,2,1,0:T(8,128)S(1)} collective-permute-done((f32[1,64,64,128]{3,2,1,0:T(8,128)S(1)}, f32[1,64,64,128]{3,2,1,0:T(8,128)S(1)}, u32[]{:S(2)}, u32[]{:S(2)}) %collective-permute-start.18) | collective-permute-done | bytes 2097184 | tf_op jit(solution)/shard_map/ppermute | solution.py:17
  295.8 4.0 collective-permute-done.19
  299.7 24.8 %fusion.5 = f32[4,64,64,128]{3,2,1,0:T(8,128)} fusion(f32[4,64,64,128]{3,2,1,0:T(8,128)} %fusion.16, f32[4,64,1,128]{3,2,1,0:T(1,128)S(1)} %bitcast.30, f32[6,1,64,128]{3,2,1,0:T(8,128)S(1)} %pad.63, f32[6,1,64,128]{3,2,1,0:T(8,128)S(1)} %pad.62, f32[1,64,64,128]{3,2,1,0:T(8,128)S(1)} %collective-permute-done.19, ...), kind=kLoop, calls=%fused_computation.7 | loop fusion | flops 79691776 | bytes 30015488 | tf_op jit(solution)/shard_map/add | solution.py:59
  324.5 8.7 %fusion.56 = f32[4,64,64,128]{3,2,1,0:T(8,128)} fusion(f32[4,64,64,128]{3,2,1,0:T(8,128)} %fusion.5), kind=kOutput, calls=%fused_computation.127 | output fusion | flops 6291456 | bytes 16777216 | tf_op jit(solution)/shard_map/jit(cumsum)/reduce_window_sum | solution.py:66
  333.2 3.2 slice.370
  336.5 86.6 %all-gather.3.cloned.1.call-done = f32[4,64,64,128]{3,2,1,0:T(8,128)} async-done(((f32[1,64,64,128]{3,2,1,0:T(8,128)}), f32[4,64,64,128]{3,2,1,0:T(8,128)}) %all-gather.3.cloned.1.call-update) | async-done | bytes 8388624 | tf_op jit(solution)/shard_map/all_gather | solution.py:31
  423.1 9.3 %while.14 = (s32[]{:T(128)}, f32[1,64,64,128]{3,2,1,0:T(8,128)S(1)}, s32[]{:T(128)}, f32[4,1,64,64,128]{4,3,2,1,0:T(8,128)}, s32[]{:T(128)}, /*index=5*/s32[]{:T(128)}) while((s32[]{:T(128)}, f32[1,64,64,128]{3,2,1,0:T(8,128)S(1)}, s32[]{:T(128)}, f32[4,1,64,64,128]{4,3,2,1,0:T(8,128)}, s32[]{:T(128)}, /*index=5*/s32[]{:T(128)}) %tuple.57), condition=%wide.region_2.3_spmd.clone, body=%wide.region_1.2_spmd.clone.sunk | while | flops 1572868 | bytes 6291549 | solution.py:39
  432.5 8.8 %add_multiply_fusion = f32[4,64,64,128]{3,2,1,0:T(8,128)} fusion(f32[4,64,64,128]{3,2,1,0:T(8,128)} %fusion.56, f32[64,64,128]{2,1,0:T(8,128)S(1)} %bitcast.27), kind=kLoop, calls=%fused_computation.111 | loop fusion | flops 4194304 | bytes 18874368 | tf_op jit(solution)/shard_map/div | solution.py:73
  (60 shorter events, 51.9 us)
Async XLA Ops:
  7.2 416.0 %all-gather.3.cloned.1.call-start = ((), (), s32[]{:S(2)}) async-start(), calls=%async_computation | async-start | bytes 10485760 | tf_op jit(solution)/shard_map/all_gather | solution.py:31
  9.7 48.7 %collective-permute-start = (f32[1,64,64,128]{3,2,1,0:T(8,128)S(1)}, f32[1,64,64,128]{3,2,1,0:T(8,128)S(1)}, u32[]{:S(2)}, u32[]{:S(2)}) collective-permute-start(f32[1,64,64,128]{3,2,1,0:T(8,128)S(1)} %get-tuple-element.142), channel_id=1, source_target_pairs={{0,32},{32,64},{64,96},{1,33},{33,65},{65,97},{2,34},{34,66},{66,9... | collective-permute-start | bytes 6291464 | tf_op jit(solution)/shard_map/ppermute | solution.py:17
  14.2 54.6 %collective-permute-start.1 = (f32[1,64,64,128]{3,2,1,0:T(8,128)S(1)}, f32[1,64,64,128]{3,2,1,0:T(8,128)S(1)}, u32[]{:S(2)}, u32[]{:S(2)}) collective-permute-start(f32[1,64,64,128]{3,2,1,0:T(8,128)S(1)} %get-tuple-element.141), channel_id=1, source_target_pairs={{32,0},{64,32},{96,64},{33,1},{65,33},{97,65},{34,2},{66,34},{98,6... | collective-permute-start | bytes 6291464 | tf_op jit(solution)/shard_map/ppermute | solution.py:18
  16.5 10.5 %collective-permute-start.2 = (f32[4,1,64,128]{3,2,1,0:T(8,128)S(1)}, f32[4,1,64,128]{3,2,1,0:T(8,128)S(1)}, u32[]{:S(2)}, u32[]{:S(2)}) collective-permute-start(f32[4,1,64,128]{3,2,1,0:T(8,128)S(1)} %get-tuple-element.139), channel_id=1, source_target_pairs={{0,4},{4,8},{8,12},{12,16},{16,20},{20,24},{24,28},{1,5},{5,9},{9,... | collective-permute-start | bytes 393224 | tf_op jit(solution)/shard_map/ppermute | solution.py:17
  19.7 9.3 %collective-permute-start.3 = (f32[4,1,64,128]{3,2,1,0:T(8,128)S(1)}, f32[4,1,64,128]{3,2,1,0:T(8,128)S(1)}, u32[]{:S(2)}, u32[]{:S(2)}) collective-permute-start(f32[4,1,64,128]{3,2,1,0:T(8,128)S(1)} %get-tuple-element.140), channel_id=1, source_target_pairs={{4,0},{8,4},{12,8},{16,12},{20,16},{24,20},{28,24},{5,1},{9,5},{13... | collective-permute-start | bytes 393224 | tf_op jit(solution)/shard_map/ppermute | solution.py:18
  22.7 47.8 %collective-permute-start.4 = (f32[4,64,1,128]{3,1,2,0:T(8,128)S(1)}, f32[4,64,1,128]{3,1,2,0:T(8,128)S(1)}, u32[]{:S(2)}, u32[]{:S(2)}) collective-permute-start(f32[4,64,1,128]{3,1,2,0:T(8,128)S(1)} %bitcast.38), channel_id=1, source_target_pairs={{0,1},{1,2},{2,3},{4,5},{5,6},{6,7},{8,9},{9,10},{10,11},{12,13},{... | collective-permute-start | bytes 393224 | tf_op jit(solution)/shard_map/ppermute | solution.py:17
  27.1 43.5 %collective-permute-start.5 = (f32[4,64,1,128]{3,1,2,0:T(8,128)S(1)}, f32[4,64,1,128]{3,1,2,0:T(8,128)S(1)}, u32[]{:S(2)}, u32[]{:S(2)}) collective-permute-start(f32[4,64,1,128]{3,1,2,0:T(8,128)S(1)} %bitcast.37), channel_id=1, source_target_pairs={{1,0},{2,1},{3,2},{5,4},{6,5},{7,6},{9,8},{10,9},{11,10},{13,12},{... | collective-permute-start | bytes 393224 | tf_op jit(solution)/shard_map/ppermute | solution.py:18
  58.4 12.1 %slice-start = ((s8[8388608]{0:T(1024)(128)(4,1)}), s8[4194304]{0:T(1024)(128)(4,1)S(1)}, s32[]{:S(2)}) async-start(s8[8388608]{0:T(1024)(128)(4,1)} %bitcast.25), calls=%async_computation.1 | async-start | bytes 8388608
  60.0 10.5 %slice-start.1 = ((s8[8388608]{0:T(1024)(128)(4,1)}), s8[4194304]{0:T(1024)(128)(4,1)S(1)}, s32[]{:S(2)}) async-start(s8[8388608]{0:T(1024)(128)(4,1)} %bitcast.25), calls=%async_computation.2 | async-start | bytes 8388608
  95.7 47.6 %collective-permute-start.6 = (f32[1,64,64,128]{3,2,1,0:T(8,128)S(1)}, f32[1,64,64,128]{3,2,1,0:T(8,128)S(1)}, u32[]{:S(2)}, u32[]{:S(2)}) collective-permute-start(f32[1,64,64,128]{3,2,1,0:T(8,128)S(1)} %get-tuple-element.133), channel_id=1, source_target_pairs={{0,32},{32,64},{64,96},{1,33},{33,65},{65,97},{2,34},{34,66},{66,9... | collective-permute-start | bytes 6291464 | tf_op jit(solution)/shard_map/ppermute | solution.py:17
  100.0 47.4 %collective-permute-start.7 = (f32[1,64,64,128]{3,2,1,0:T(8,128)S(1)}, f32[1,64,64,128]{3,2,1,0:T(8,128)S(1)}, u32[]{:S(2)}, u32[]{:S(2)}) collective-permute-start(f32[1,64,64,128]{3,2,1,0:T(8,128)S(1)} %get-tuple-element.134), channel_id=1, source_target_pairs={{32,0},{64,32},{96,64},{33,1},{65,33},{97,65},{34,2},{66,34},{98,6... | collective-permute-start | bytes 6291464 | tf_op jit(solution)/shard_map/ppermute | solution.py:18
  102.3 11.4 %collective-permute-start.8 = (f32[4,1,64,128]{3,2,1,0:T(8,128)S(1)}, f32[4,1,64,128]{3,2,1,0:T(8,128)S(1)}, u32[]{:S(2)}, u32[]{:S(2)}) collective-permute-start(f32[4,1,64,128]{3,2,1,0:T(8,128)S(1)} %get-tuple-element.135), channel_id=1, source_target_pairs={{0,4},{4,8},{8,12},{12,16},{16,20},{20,24},{24,28},{1,5},{5,9},{9,... | collective-permute-start | bytes 393224 | tf_op jit(solution)/shard_map/ppermute | solution.py:17
  105.4 10.2 %collective-permute-start.9 = (f32[4,1,64,128]{3,2,1,0:T(8,128)S(1)}, f32[4,1,64,128]{3,2,1,0:T(8,128)S(1)}, u32[]{:S(2)}, u32[]{:S(2)}) collective-permute-start(f32[4,1,64,128]{3,2,1,0:T(8,128)S(1)} %get-tuple-element.136), channel_id=1, source_target_pairs={{4,0},{8,4},{12,8},{16,12},{20,16},{24,20},{28,24},{5,1},{9,5},{13... | collective-permute-start | bytes 393224 | tf_op jit(solution)/shard_map/ppermute | solution.py:18
  108.5 7.2 %collective-permute-start.10 = (f32[4,64,1,128]{3,1,2,0:T(8,128)S(1)}, f32[4,64,1,128]{3,1,2,0:T(8,128)S(1)}, u32[]{:S(2)}, u32[]{:S(2)}) collective-permute-start(f32[4,64,1,128]{3,1,2,0:T(8,128)S(1)} %bitcast.43), channel_id=1, source_target_pairs={{0,1},{1,2},{2,3},{4,5},{5,6},{6,7},{8,9},{9,10},{10,11},{12,13},{... | collective-permute-start | bytes 393224 | tf_op jit(solution)/shard_map/ppermute | solution.py:17
  113.7 6.6 %collective-permute-start.11 = (f32[4,64,1,128]{3,1,2,0:T(8,128)S(1)}, f32[4,64,1,128]{3,1,2,0:T(8,128)S(1)}, u32[]{:S(2)}, u32[]{:S(2)}) collective-permute-start(f32[4,64,1,128]{3,1,2,0:T(8,128)S(1)} %bitcast.40), channel_id=1, source_target_pairs={{1,0},{2,1},{3,2},{5,4},{6,5},{7,6},{9,8},{10,9},{11,10},{13,12},{... | collective-permute-start | bytes 393224 | tf_op jit(solution)/shard_map/ppermute | solution.py:18
  174.7 45.6 %collective-permute-start.12 = (f32[1,64,64,128]{3,2,1,0:T(8,128)S(1)}, f32[1,64,64,128]{3,2,1,0:T(8,128)S(1)}, u32[]{:S(2)}, u32[]{:S(2)}) collective-permute-start(f32[1,64,64,128]{3,2,1,0:T(8,128)S(1)} %get-tuple-element.127), channel_id=1, source_target_pairs={{0,32},{32,64},{64,96},{1,33},{33,65},{65,97},{2,34},{34,66},{66,9... | collective-permute-start | bytes 6291464 | tf_op jit(solution)/shard_map/ppermute | solution.py:17
  178.2 46.1 %collective-permute-start.13 = (f32[1,64,64,128]{3,2,1,0:T(8,128)S(1)}, f32[1,64,64,128]{3,2,1,0:T(8,128)S(1)}, u32[]{:S(2)}, u32[]{:S(2)}) collective-permute-start(f32[1,64,64,128]{3,2,1,0:T(8,128)S(1)} %get-tuple-element.128), channel_id=1, source_target_pairs={{32,0},{64,32},{96,64},{33,1},{65,33},{97,65},{34,2},{66,34},{98,6... | collective-permute-start | bytes 6291464 | tf_op jit(solution)/shard_map/ppermute | solution.py:18
  180.5 12.5 %collective-permute-start.14 = (f32[4,1,64,128]{3,2,1,0:T(8,128)S(1)}, f32[4,1,64,128]{3,2,1,0:T(8,128)S(1)}, u32[]{:S(2)}, u32[]{:S(2)}) collective-permute-start(f32[4,1,64,128]{3,2,1,0:T(8,128)S(1)} %get-tuple-element.129), channel_id=1, source_target_pairs={{0,4},{4,8},{8,12},{12,16},{16,20},{20,24},{24,28},{1,5},{5,9},{9,... | collective-permute-start | bytes 393224 | tf_op jit(solution)/shard_map/ppermute | solution.py:17
  183.6 11.5 %collective-permute-start.15 = (f32[4,1,64,128]{3,2,1,0:T(8,128)S(1)}, f32[4,1,64,128]{3,2,1,0:T(8,128)S(1)}, u32[]{:S(2)}, u32[]{:S(2)}) collective-permute-start(f32[4,1,64,128]{3,2,1,0:T(8,128)S(1)} %get-tuple-element.130), channel_id=1, source_target_pairs={{4,0},{8,4},{12,8},{16,12},{20,16},{24,20},{28,24},{5,1},{9,5},{13... | collective-permute-start | bytes 393224 | tf_op jit(solution)/shard_map/ppermute | solution.py:18
  186.7 8.5 %collective-permute-start.16 = (f32[4,64,1,128]{3,1,2,0:T(8,128)S(1)}, f32[4,64,1,128]{3,1,2,0:T(8,128)S(1)}, u32[]{:S(2)}, u32[]{:S(2)}) collective-permute-start(f32[4,64,1,128]{3,1,2,0:T(8,128)S(1)} %bitcast.44), channel_id=1, source_target_pairs={{0,1},{1,2},{2,3},{4,5},{5,6},{6,7},{8,9},{9,10},{10,11},{12,13},{... | collective-permute-start | bytes 393224 | tf_op jit(solution)/shard_map/ppermute | solution.py:17
  193.0 6.6 %collective-permute-start.17 = (f32[4,64,1,128]{3,1,2,0:T(8,128)S(1)}, f32[4,64,1,128]{3,1,2,0:T(8,128)S(1)}, u32[]{:S(2)}, u32[]{:S(2)}) collective-permute-start(f32[4,64,1,128]{3,1,2,0:T(8,128)S(1)} %bitcast.41), channel_id=1, source_target_pairs={{1,0},{2,1},{3,2},{5,4},{6,5},{7,6},{9,8},{10,9},{11,10},{13,12},{... | collective-permute-start | bytes 393224 | tf_op jit(solution)/shard_map/ppermute | solution.py:18
  251.5 44.3 %collective-permute-start.18 = (f32[1,64,64,128]{3,2,1,0:T(8,128)S(1)}, f32[1,64,64,128]{3,2,1,0:T(8,128)S(1)}, u32[]{:S(2)}, u32[]{:S(2)}) collective-permute-start(f32[1,64,64,128]{3,2,1,0:T(8,128)S(1)} %get-tuple-element.121), channel_id=1, source_target_pairs={{0,32},{32,64},{64,96},{1,33},{33,65},{65,97},{2,34},{34,66},{66,9... | collective-permute-start | bytes 6291464 | tf_op jit(solution)/shard_map/ppermute | solution.py:17
  254.7 45.0 %collective-permute-start.19 = (f32[1,64,64,128]{3,2,1,0:T(8,128)S(1)}, f32[1,64,64,128]{3,2,1,0:T(8,128)S(1)}, u32[]{:S(2)}, u32[]{:S(2)}) collective-permute-start(f32[1,64,64,128]{3,2,1,0:T(8,128)S(1)} %get-tuple-element.122), channel_id=1, source_target_pairs={{32,0},{64,32},{96,64},{33,1},{65,33},{97,65},{34,2},{66,34},{98,6... | collective-permute-start | bytes 6291464 | tf_op jit(solution)/shard_map/ppermute | solution.py:18
  257.0 12.5 %collective-permute-start.20 = (f32[4,1,64,128]{3,2,1,0:T(8,128)S(1)}, f32[4,1,64,128]{3,2,1,0:T(8,128)S(1)}, u32[]{:S(2)}, u32[]{:S(2)}) collective-permute-start(f32[4,1,64,128]{3,2,1,0:T(8,128)S(1)} %get-tuple-element.123), channel_id=1, source_target_pairs={{0,4},{4,8},{8,12},{12,16},{16,20},{20,24},{24,28},{1,5},{5,9},{9,... | collective-permute-start | bytes 393224 | tf_op jit(solution)/shard_map/ppermute | solution.py:17
  260.1 12.5 %collective-permute-start.21 = (f32[4,1,64,128]{3,2,1,0:T(8,128)S(1)}, f32[4,1,64,128]{3,2,1,0:T(8,128)S(1)}, u32[]{:S(2)}, u32[]{:S(2)}) collective-permute-start(f32[4,1,64,128]{3,2,1,0:T(8,128)S(1)} %get-tuple-element.124), channel_id=1, source_target_pairs={{4,0},{8,4},{12,8},{16,12},{20,16},{24,20},{28,24},{5,1},{9,5},{13... | collective-permute-start | bytes 393224 | tf_op jit(solution)/shard_map/ppermute | solution.py:18
  263.2 10.4 %collective-permute-start.23 = (f32[4,64,1,128]{3,1,2,0:T(8,128)S(1)}, f32[4,64,1,128]{3,1,2,0:T(8,128)S(1)}, u32[]{:S(2)}, u32[]{:S(2)}) collective-permute-start(f32[4,64,1,128]{3,1,2,0:T(8,128)S(1)} %bitcast.42), channel_id=1, source_target_pairs={{1,0},{2,1},{3,2},{5,4},{6,5},{7,6},{9,8},{10,9},{11,10},{13,12},{... | collective-permute-start | bytes 393224 | tf_op jit(solution)/shard_map/ppermute | solution.py:18
  269.5 5.0 %collective-permute-start.22 = (f32[4,64,1,128]{3,1,2,0:T(8,128)S(1)}, f32[4,64,1,128]{3,1,2,0:T(8,128)S(1)}, u32[]{:S(2)}, u32[]{:S(2)}) collective-permute-start(f32[4,64,1,128]{3,1,2,0:T(8,128)S(1)} %bitcast.39), channel_id=1, source_target_pairs={{0,1},{1,2},{2,3},{4,5},{5,6},{6,7},{8,9},{9,10},{10,11},{12,13},{... | collective-permute-start | bytes 393224 | tf_op jit(solution)/shard_map/ppermute | solution.py:17
Sparse Core Ops, SparseCore 0:
  336.6 86.4 all-gather.2
where the time goes:
time: 449 us; the launch traced here: 448 us
  waiting for transfers between devices  204 us (45%)
  other arithmetic  124 us (28%)
  starting transfers between devices  69.4 us (15%)
  local copies, waits for them, and re-layouts  36.5 us (8%)
  between operations  14.4 us (3%)
    add x4, other arithmetic, advance(): return middle + 0.1 * spread + 0.2 * middle * (1.0 - middle * crowding)  96.9 us
    ppermute x12, waiting for transfers between devices, extended(): lax.ppermute(last, axis, up)  95.4 us
    all_gather x1, waiting for transfers between devices, prefix(): everything = lax.all_gather(array, axis)  86.6 us
    ppermute x12, starting transfers between devices, extended(): lax.ppermute(last, axis, up)  46.8 us
    ppermute x12, starting transfers between devices, extended(): lax.ppermute(initial, axis, [(b, a) for a, b in up])  22.5 us
    ppermute x12, waiting for transfers between devices, extended(): lax.ppermute(initial, axis, [(b, a) for a, b in up])  21.9 us
    slice x11, local copies, waits for them, and re-layouts, extended(): last = lax.slice_in_dim(array, length - width, length, axis=dim)  18.5 us
    unnamed x6, local copies, waits for them, and re-layouts  10.5 us
  transfers between devices with their start and end apart: 25, of which 12 were waited for; matrix products, arithmetic and copies ran while one was open for 5% of the time, Pallas kernels for 0%

commit v1 on v0

v1 whole, which is shorter than its diff:
```python
import functools

import jax
import jax.numpy as jnp
from jax import lax
from jax.experimental import pallas as pl
from jax.experimental.pallas import tpu as pltpu
from jax.sharding import PartitionSpec as P

STEPS = 4
CHUNKS = 2
PLANES = 4


def stencil(refs, chunk_x, base, masked_low):
    c, k, ylo, yhi, xlo, xhi, zlo, zhi = refs
    rows, _, zs, lanes = k.shape
    z = lax.broadcasted_iota(jnp.int32, (zs, lanes), 0)

    def plane(y, xx):
        x = base + xx
        mid = c[y, x]
        if xx == 0:
            left = jnp.where(x == 0, xlo[y, 0], c[y, jnp.maximum(x - 1, 0)])
        else:
            left = c[y, x - 1]
        if xx == k.shape[1] - 1:
            right = jnp.where(x == chunk_x - 1, xhi[y, 0], c[y, jnp.minimum(x + 1, chunk_x - 1)])
        else:
            right = c[y, x + 1]
        down = jnp.where(z == 0, zlo[y, xx], pltpu.roll(mid, 1, 0))
        up = jnp.where(z == zs - 1, zhi[y, xx], pltpu.roll(mid, zs - 1, 0))
        if y > 0:
            before = c[y - 1, x]
        elif ylo is None:
            before = masked_low * mid
        else:
            before = ylo[xx]
        if y < rows - 1:
            after = c[y + 1, x]
        elif yhi is None:
            after = mid
        else:
            after = yhi[xx]
        around = ((before + after) + (left + right)) + (down + up)
        return mid * (0.6 - (0.2 * mid) * k[y, xx]) + 0.1 * around

    return plane


def step_kernel(c, k, ylo, yhi, xlo, xhi, zlo, zhi, out, row_lo, row_hi, zlo_out, zhi_out, edge, *, chunk_x, edge_x):
    i = pl.program_id(0)
    rows, planes, zs, _ = k.shape
    plane = stencil((c, k, ylo, yhi, xlo, xhi, zlo, zhi), chunk_x, i * planes, None)
    for xx in range(planes):
        for y in range(rows):
            new = plane(y, xx)
            out[y, xx] = new
            zlo_out[y, xx] = new[0:1]
            zhi_out[y, xx] = new[zs - 1 : zs]
            if y == 0:
                row_lo[xx] = new
            if y == rows - 1:
                row_hi[xx] = new
            if edge_x is not None and edge_x % planes == xx:

                @pl.when(i == edge_x // planes)
                def _():
                    edge[y, 0] = new


def total_kernel(place, c, k, xlo, xhi, zlo, zhi, total, *, chunk_x):
    i = pl.program_id(0)
    rows, planes, _, _ = k.shape
    inside = jnp.where(place[0] > 0, 1.0, 0.0).astype(jnp.float32)
    plane = stencil((c, k, None, None, xlo, xhi, zlo, zhi), chunk_x, i * planes, inside)
    for xx in range(planes):
        value = plane(0, xx)
        for y in range(1, rows):
            value = value + plane(y, xx)
        total[xx] = value


def last_kernel(place, c, k, ylo, yhi, xlo, xhi, zlo, zhi, *rest, chunk_x):
    out, sums = rest[-2:]
    i = pl.program_id(0)
    rows, planes, _, _ = k.shape
    inside = jnp.where(place[0] > 0, 0.1, 0.0).astype(jnp.float32)
    plane = stencil((c, k, ylo, yhi, xlo, xhi, zlo, zhi), chunk_x, i * planes, None)
    for xx in range(planes):
        sofar = inside * c[0, i * planes + xx] - 0.1 * ylo[xx]
        for y in range(rows):
            new = plane(y, xx)
            out[y, xx] = new
            sofar = sofar + new
            sums[y, xx] = sofar


def add_kernel(place, sums, one, two, three, *rest, scale):
    out = rest[-1]
    rows, planes, _, _ = sums.shape
    inside = jnp.where(place[0] > 0, 1.0, 0.0).astype(jnp.float32)
    for xx in range(planes):
        below = one[xx] + inside * two[xx] + three[xx]
        for y in range(rows):
            out[y, xx] = (sums[y, xx] + below) * scale


class Source:
    def __init__(self, array, start, length):
        self.array, self.start, self.length = array, start, length

    def whole(self):
        rows, _, zs, lanes = self.array.shape
        at = self.start // self.length
        return pl.BlockSpec((rows, self.length, zs, lanes), lambda i: (0, at, 0, 0))

    def stepped(self, planes):
        rows, _, zs, lanes = self.array.shape
        at = self.start // planes
        return pl.BlockSpec((rows, planes, zs, lanes), lambda i: (0, at + i, 0, 0))

    def plane(self, x):
        rows, _, zs, lanes = self.array.shape
        at = self.start + x
        return pl.BlockSpec((rows, 1, zs, lanes), lambda i: (0, at, 0, 0))


def rows_spec(planes, zs, lanes):
    return pl.BlockSpec((planes, zs, lanes), lambda i: (i, 0, 0))


def edge_spec(rows, planes, lanes):
    return pl.BlockSpec((rows, planes, 1, lanes), lambda i: (0, i, 0, 0))


def cost(cells, per_cell):
    return pl.CostEstimate(flops=cells * per_cell, bytes_accessed=cells * 12, transcendentals=0)


SMEM = pl.BlockSpec(memory_space=pltpu.SMEM)
ANY = pl.BlockSpec(memory_space=pl.ANY)


def shifts(axis):
    count = lax.axis_size(axis)
    up = [(i, i + 1) for i in range(count - 1)]
    return up, [(b, a) for a, b in up]


def body(tracer, crowding):
    rows, xs, zs, lanes = tracer.shape
    n = CHUNKS
    size = xs // n
    planes = PLANES
    grid = (size // planes,)
    cells = rows * size * zs * lanes
    f32 = jnp.float32
    place = lax.axis_index("rows").astype(jnp.int32).reshape(1)
    row_up, row_down = shifts("rows")
    col_up, col_down = shifts("cols")
    slab_up, slab_down = shifts("slabs")
    params = pltpu.CompilerParams(dimension_semantics=("arbitrary",), vmem_limit_bytes=40 * 2**20)
    row_block = rows_spec(planes, zs, lanes)
    edge_block = edge_spec(rows, planes, lanes)
    row_shape = jax.ShapeDtypeStruct((size, zs, lanes), f32)
    edge_shape = jax.ShapeDtypeStruct((rows, size, 1, lanes), f32)

    field = [Source(tracer, j * size, size) for j in range(n)]
    crowd = [Source(crowding, j * size, size) for j in range(n)]

    def exchange_rows(lo, hi):
        return (lax.ppermute(hi, "rows", row_up), lax.ppermute(lo, "rows", row_down))

    def exchange_z(lo, hi):
        return (lax.ppermute(hi, "slabs", slab_up), lax.ppermute(lo, "slabs", slab_down))

    halo_y = [
        exchange_rows(tracer[0, j * size : (j + 1) * size], tracer[rows - 1, j * size : (j + 1) * size]) for j in range(n)
    ]
    halo_x = (lax.ppermute(tracer[:, xs - 1 : xs], "cols", col_up), lax.ppermute(tracer[:, 0:1], "cols", col_down))
    zlo_all, zhi_all = tracer[:, :, 0:1], tracer[:, :, zs - 1 : zs]
    z_all = exchange_z(zlo_all, zhi_all)
    halo_z = [(z_all[0][:, j * size : (j + 1) * size], z_all[1][:, j * size : (j + 1) * size]) for j in range(n)]

    def x_sides(field, halo_x, j):
        low = (halo_x[0], pl.BlockSpec((rows, 1, zs, lanes), lambda i: (0, 0, 0, 0))) if j == 0 else (field[j - 1].array, field[j - 1].plane(size - 1))
        high = (
            (halo_x[1], pl.BlockSpec((rows, 1, zs, lanes), lambda i: (0, 0, 0, 0)))
            if j == n - 1
            else (field[j + 1].array, field[j + 1].plane(0))
        )
        return low, high

    for step in range(STEPS - 1):
        made, next_y, next_z, edges = [], [], [], {}
        for j in range(n):
            low, high = x_sides(field, halo_x, j)
            edge_x = {0: 0, n - 1: size - 1}.get(j)
            out, lo, hi, zlo, zhi, edge = pl.pallas_call(
                functools.partial(step_kernel, chunk_x=size, edge_x=edge_x),
                grid=grid,
                in_specs=[field[j].whole(), crowd[j].stepped(planes), row_block, row_block, low[1], high[1], edge_block, edge_block],
                out_specs=[
                    pl.BlockSpec((rows, planes, zs, lanes), lambda i: (0, i, 0, 0)),
                    row_block,
                    row_block,
                    edge_block,
                    edge_block,
                    pl.BlockSpec((rows, 1, zs, lanes), lambda i: (0, 0, 0, 0)),
                ],
                out_shape=[
                    jax.ShapeDtypeStruct((rows, size, zs, lanes), f32),
                    row_shape,
                    row_shape,
                    edge_shape,
                    edge_shape,
                    jax.ShapeDtypeStruct((rows, 1, zs, lanes), f32),
                ],
                compiler_params=params,
                cost_estimate=cost(cells, 14),
                name=f"step{step}_{j}",
            )(field[j].array, crowd[j].array, *halo_y[j], low[0], high[0], *halo_z[j])
            made.append(Source(out, 0, size))
            next_y.append(exchange_rows(lo, hi))
            next_z.append(exchange_z(zlo, zhi))
            edges[j] = edge
        halo_x = (lax.ppermute(edges[n - 1], "cols", col_up), lax.ppermute(edges[0], "cols", col_down))
        field, halo_y, halo_z = made, next_y, next_z

    one, two, three = [], [], []
    for j in range(n):
        low, high = x_sides(field, halo_x, j)
        total = pl.pallas_call(
            functools.partial(total_kernel, chunk_x=size),
            grid=grid,
            in_specs=[SMEM, field[j].whole(), crowd[j].stepped(planes), low[1], high[1], edge_block, edge_block],
            out_specs=row_block,
            out_shape=row_shape,
            compiler_params=params,
            cost_estimate=cost(cells, 14),
            name=f"total_{j}",
        )(place, field[j].array, crowd[j].array, low[0], high[0], *halo_z[j])
        two.append(lax.ppermute(total, "rows", [(0, 3), (1, 0)]))
        one.append(lax.ppermute(total, "rows", row_up))
        three.append(lax.ppermute(two[j], "rows", [(3, 2), (0, 3)]))

    full = jax.ShapeDtypeStruct(tracer.shape, f32)
    end = None
    sums = []
    for j in range(n):
        low, high = x_sides(field, halo_x, j)
        operands = [place, field[j].array, crowd[j].array, *halo_y[j], low[0], high[0], *halo_z[j]]
        specs = [SMEM, field[j].whole(), crowd[j].stepped(planes), row_block, row_block, low[1], high[1], edge_block, edge_block]
        alias = {}
        if end is not None:
            alias = {len(operands): 0}
            operands.append(end)
            specs.append(ANY)
        end, partial = pl.pallas_call(
            functools.partial(last_kernel, chunk_x=size),
            grid=grid,
            in_specs=specs,
            out_specs=[
                pl.BlockSpec((rows, planes, zs, lanes), lambda i, j=j: (0, j * grid[0] + i, 0, 0)),
                pl.BlockSpec((rows, planes, zs, lanes), lambda i: (0, i, 0, 0)),
            ],
            out_shape=[full, jax.ShapeDtypeStruct((rows, size, zs, lanes), f32)],
            input_output_aliases=alias,
            compiler_params=params,
            cost_estimate=cost(cells, 18),
            name=f"last_{j}",
        )(*operands)
        sums.append(partial)

    column = None
    for j in range(n):
        operands = [place, sums[j], one[j], two[j], three[j]]
        block = pl.BlockSpec((rows, planes, zs, lanes), lambda i: (0, i, 0, 0))
        specs = [SMEM, block, row_block, row_block, row_block]
        alias = {}
        if column is not None:
            alias = {len(operands): 0}
            operands.append(column)
            specs.append(ANY)
        column = pl.pallas_call(
            functools.partial(add_kernel, scale=1.0 / (rows * lax.axis_size("rows"))),
            grid=grid,
            in_specs=specs,
            out_specs=pl.BlockSpec((rows, planes, zs, lanes), lambda i, j=j: (0, j * grid[0] + i, 0, 0)),
            out_shape=full,
            input_output_aliases=alias,
            compiler_params=params,
            cost_estimate=cost(cells, 3),
            name=f"add_{j}",
        )(*operands)
    return column, end


def solution(mesh):
    spec = P("rows", "cols", "slabs", None)
    return jax.shard_map(body, mesh=mesh, in_specs=(spec, spec), out_specs=(spec, spec), check_vma=False)
```

time: 449 us -> 324 us (0.72)
  other arithmetic: 124 us -> 0 us
  waiting for transfers between devices: 204 us -> 92.8 us
  Pallas kernels: 0 us -> 81.7 us
  starting transfers between devices: 69.4 us -> 121 us
  local copies, waits for them, and re-layouts: 36.5 us -> 22.3 us
  between operations: 14.4 us -> 1.33 us
    add x4 -> x0, other arithmetic: 96.9 us -> none  [advance(): return middle + 0.1 * spread + 0.2 * middle * (1.0 - middle * crowding)]
    all_gather x1 -> x0, waiting for transfers between devices: 86.6 us -> none  [prefix(): everything = lax.all_gather(array, axis)]
    pallas_call x0 -> x12, Pallas kernels: none -> 81.7 us  [the longest x6 43.1 us: body(): pl.pallas_call(functools.partial(step_kernel, chunk_x=size, edge_x=edge_x...]
    ppermute x24 -> x44, starting transfers between devices: 69.4 us -> 121 us  [the longest x8 32 us: exchange_rows(): lax.ppermute(hi, 'rows', row_up)]
    ppermute x24 -> x44, waiting for transfers between devices: 117 us -> 92.8 us  [the longest x2 34 us: body(): two.append(lax.ppermute(total, 'rows', [(0, 3), (1, 0)]))]
    slice x13 -> x4, local copies, waits for them, and re-layouts: 24.3 us -> 2.76 us  [the longest x1 1.74 us: body(): zlo_all, zhi_all = (tracer[:, :, 0:1], tracer[:, :, zs - 1:zs])]
    select_n x4 -> x0, other arithmetic: 9.24 us -> none  [turn(): return jnp.where(reached, new, before)]
    div x1 -> x0, other arithmetic: 8.78 us -> none  [body(): column_sum = (here + below) / (tracer.shape[0] * lax.axis_size('rows'))]
  transfers between devices with their start and end apart: 25 -> 44, of which waited for: 12 -> 14; matrix products, arithmetic and copies ran while one was open for 5% -> 1% of each run, Pallas kernels for 0% -> 24%
where the time goes in v1:
time: 324 us; the launch traced here: 319 us
  starting transfers between devices  121 us (37%)
  waiting for transfers between devices  92.8 us (29%)
  Pallas kernels  81.7 us (25%)
  local copies, waits for them, and re-layouts  22.3 us (7%)
    pallas_call x6, Pallas kernels, body(): pl.pallas_call(functools.partial(step_kernel, chunk_x=size, edge_x=edge_x...  43.1 us
    ppermute x2, waiting for transfers between devices, body(): two.append(lax.ppermute(total, 'rows', [(0, 3), (1, 0)]))  34 us
    ppermute x8, starting transfers between devices, exchange_rows(): lax.ppermute(hi, 'rows', row_up)  32 us
    ppermute x7, starting transfers between devices, exchange_z(): lax.ppermute(hi, 'slabs', slab_up)  29.3 us
    unnamed x32, local copies, waits for them, and re-layouts  16.8 us
    pallas_call x2, Pallas kernels, body(): pl.pallas_call(functools.partial(last_kernel, chunk_x=size), grid=grid, i...  15.1 us
    ppermute x8, waiting for transfers between devices, exchange_rows(): lax.ppermute(hi, 'rows', row_up)  14.6 us
    ppermute x7, waiting for transfers between devices, exchange_z(): lax.ppermute(lo, 'slabs', slab_down)  14.5 us
  transfers between devices with their start and end apart: 44, of which 14 were waited for; matrix products, arithmetic and copies ran while one was open for 1% of the time, Pallas kernels for 24%

profile of v1, /device:TPU:1, one launch (start us, length us, event | category | flops | bytes accessed | tf_op | source)
XLA Modules:
  0.0 318.8 jit_solution(2200032480075530395)
XLA Ops:
  3.4 4.4 %collective-permute-start = (f32[32,64,128]{2,1,0:T(8,128)S(1)}, f32[32,64,128]{2,1,0:T(8,128)S(1)}, u32[]{:S(2)}, u32[]{:S(2)}) collective-permute-start(f32[32,64,128]{2,1,0:T(8,128)S(1)} %get-tuple-element.87), channel_id=1, source_target_pairs={{0,32},{32,64},{64,96},{1,33},{33,65},{65,97},{2,34},{34,66},{66,9... | collective-permute-start | bytes 3145736 | tf_op jit(solution)/shard_map/ppermute | solution.py:173
  9.1 4.2 %collective-permute-start.7 = (f32[32,64,128]{2,1,0:T(8,128)S(1)}, f32[32,64,128]{2,1,0:T(8,128)S(1)}, u32[]{:S(2)}, u32[]{:S(2)}) collective-permute-start(f32[32,64,128]{2,1,0:T(8,128)S(1)} %get-tuple-element.85), channel_id=1, source_target_pairs={{0,32},{32,64},{64,96},{1,33},{33,65},{65,97},{2,34},{34,66},{66,9... | collective-permute-start | bytes 3145736 | tf_op jit(solution)/shard_map/ppermute | solution.py:173
  21.6 5.3 %collective-permute-start.3 = (f32[4,64,1,128]{3,2,1,0:T(1,128)S(1)}, f32[4,64,1,128]{3,2,1,0:T(1,128)S(1)}, u32[]{:S(2)}, u32[]{:S(2)}) collective-permute-start(f32[4,64,1,128]{3,2,1,0:T(1,128)S(1)} %get-tuple-element.89), channel_id=1, source_target_pairs={{0,1},{1,2},{2,3},{4,5},{5,6},{6,7},{8,9},{9,10},{10,11},{12,13},{... | collective-permute-start | bytes 393224 | tf_op jit(solution)/shard_map/ppermute | solution.py:176
  30.8 5.3 %collective-permute-done.4 = f32[4,64,1,128]{3,2,1,0:T(1,128)S(1)} collective-permute-done((f32[4,64,1,128]{3,2,1,0:T(1,128)S(1)}, f32[4,64,1,128]{3,2,1,0:T(1,128)S(1)}, u32[]{:S(2)}, u32[]{:S(2)}) %collective-permute-start.4) | collective-permute-done | bytes 131104 | tf_op jit(solution)/shard_map/ppermute | solution.py:176
  39.3 7.5 %step0_1.1 = (f32[4,32,64,128]{3,2,1,0:T(8,128)S(1)}, f32[32,64,128]{2,1,0:T(8,128)S(1)}, f32[32,64,128]{2,1,0:T(8,128)S(1)}, f32[4,32,1,128]{3,2,1,0:T(1,128)S(...) custom-call(f32[4,64,64,128]{3,2,1,0:T(8,128)} %xhi.1, f32[4,64,64,128]{3,2,1,0:T(8,128)} %k.19, ...), custom_call_target="tpu_custom_call" | custom-call | flops 14680064 | bytes 12582912 | tf_op jit(solution)/shard_map/step0_1/pallas_call | solution.py:200
  46.9 4.3 %collective-permute-start.5 = (f32[32,64,128]{2,1,0:T(8,128)S(1)}, f32[32,64,128]{2,1,0:T(8,128)S(1)}, u32[]{:S(2)}, u32[]{:S(2)}) collective-permute-start(f32[32,64,128]{2,1,0:T(8,128)S(1)} %get-tuple-element.43), channel_id=1, source_target_pairs={{0,32},{32,64},{64,96},{1,33},{33,65},{65,97},{2,34},{34,66},{66,9... | collective-permute-start | bytes 3145736 | tf_op jit(solution)/shard_map/ppermute | solution.py:173
  56.2 7.5 %step0_0.1 = (f32[4,32,64,128]{3,2,1,0:T(8,128)S(1)}, f32[32,64,128]{2,1,0:T(8,128)S(1)}, f32[32,64,128]{2,1,0:T(8,128)S(1)}, f32[4,32,1,128]{3,2,1,0:T(1,128)S(...) custom-call(f32[4,64,64,128]{3,2,1,0:T(8,128)} %xhi.1, f32[4,64,64,128]{3,2,1,0:T(8,128)} %k.19, ...), custom_call_target="tpu_custom_call" | custom-call | flops 14680064 | bytes 12582912 | tf_op jit(solution)/shard_map/step0_0/pallas_call | solution.py:200
  70.3 6.6 %collective-permute-start.11 = (f32[4,32,1,128]{3,2,1,0:T(1,128)S(1)}, f32[4,32,1,128]{3,2,1,0:T(1,128)S(1)}, u32[]{:S(2)}, u32[]{:S(2)}) collective-permute-start(f32[4,32,1,128]{3,2,1,0:T(1,128)S(1)} %get-tuple-element.47), channel_id=1, source_target_pairs={{0,1},{1,2},{2,3},{4,5},{5,6},{6,7},{8,9},{9,10},{10,11},{12,13},{... | collective-permute-start | bytes 196616 | tf_op jit(solution)/shard_map/ppermute | solution.py:176
  80.1 4.6 %collective-permute-done.12.zhi = f32[4,32,1,128]{3,2,1,0:T(1,128)S(1)} collective-permute-done((f32[4,32,1,128]{3,2,1,0:T(1,128)S(1)}, f32[4,32,1,128]{3,2,1,0:T(1,128)S(1)}, u32[]{:S(2)}, u32[]{:S(2)}) %collective-permute-start.12) | collective-permute-done | bytes 65568 | tf_op jit(solution)/shard_map/ppermute | solution.py:176
  86.0 4.7 %collective-permute-done.10.xhi = f32[4,1,64,128]{3,2,1,0:T(8,128)S(1)} collective-permute-done((f32[4,1,64,128]{3,2,1,0:T(8,128)S(1)}, f32[4,1,64,128]{3,2,1,0:T(8,128)S(1)}, u32[]{:S(2)}, u32[]{:S(2)}) %collective-permute-start.10) | collective-permute-done | bytes 131104 | tf_op jit(solution)/shard_map/ppermute | solution.py:228
  98.5 7.5 %step1_1.1 = (f32[4,32,64,128]{3,2,1,0:T(8,128)S(1)}, f32[32,64,128]{2,1,0:T(8,128)}, f32[32,64,128]{2,1,0:T(8,128)}, f32[4,32,1,128]{3,2,1,0:T(1,128)S(1)}, f32...) custom-call(f32[4,32,64,128]{3,2,1,0:T(8,128)S(1)} %get-tuple-element.42.c.xhi, f32[4,64,64,128]{3,2,1,0:T(8,128)} %k.19, ...), custom_call_target="tpu_custom_call" | custom-call | flops 14680064 | bytes 12582912 | tf_op jit(solution)/shard_map/step1_1/pallas_call | solution.py:200
  105.9 4.3 %collective-permute-start.13 = (f32[32,64,128]{2,1,0:T(8,128)}, f32[32,64,128]{2,1,0:T(8,128)S(1)}, u32[]{:S(2)}, u32[]{:S(2)}) collective-permute-start(f32[32,64,128]{2,1,0:T(8,128)} %get-tuple-element.50), channel_id=1, source_target_pairs={{0,32},{32,64},{64,96},{1,33},{33,65},{65,97},{2,34},{34,66},{66,9... | collective-permute-start | bytes 3145736 | tf_op jit(solution)/shard_map/ppermute | solution.py:173
  111.6 6.2 %step1_0.1 = (f32[4,32,64,128]{3,2,1,0:T(8,128)S(1)}, f32[32,64,128]{2,1,0:T(8,128)S(1)}, f32[32,64,128]{2,1,0:T(8,128)S(1)}, f32[4,32,1,128]{3,2,1,0:T(1,128)S(...) custom-call(f32[4,32,64,128]{3,2,1,0:T(8,128)S(1)} %copy-done.9, f32[4,64,64,128]{3,2,1,0:T(8,128)} %k.19, ...), custom_call_target="tpu_custom_call" | custom-call | flops 14680064 | bytes 12582912 | tf_op jit(solution)/shard_map/step1_0/pallas_call | solution.py:200
  119.8 4.0 %collective-permute-start.25 = (f32[32,64,128]{2,1,0:T(8,128)S(1)}, f32[32,64,128]{2,1,0:T(8,128)S(1)}, u32[]{:S(2)}, u32[]{:S(2)}) collective-permute-start(f32[32,64,128]{2,1,0:T(8,128)S(1)} %get-tuple-element.64), channel_id=1, source_target_pairs={{0,32},{32,64},{64,96},{1,33},{33,65},{65,97},{2,34},{34,66},{66,9... | collective-permute-start | bytes 3145736 | tf_op jit(solution)/shard_map/ppermute | solution.py:173
  125.2 4.5 %collective-permute-start.21 = (f32[4,32,1,128]{3,2,1,0:T(1,128)S(1)}, f32[4,32,1,128]{3,2,1,0:T(1,128)S(1)}, u32[]{:S(2)}, u32[]{:S(2)}) collective-permute-start(f32[4,32,1,128]{3,2,1,0:T(1,128)S(1)} %get-tuple-element.59), channel_id=1, source_target_pairs={{0,1},{1,2},{2,3},{4,5},{5,6},{6,7},{8,9},{9,10},{10,11},{12,13},{... | collective-permute-start | bytes 196616 | tf_op jit(solution)/shard_map/ppermute | solution.py:176
  132.9 4.6 %collective-permute-done.22.zhi = f32[4,32,1,128]{3,2,1,0:T(1,128)S(1)} collective-permute-done((f32[4,32,1,128]{3,2,1,0:T(1,128)S(1)}, f32[4,32,1,128]{3,2,1,0:T(1,128)S(1)}, u32[]{:S(2)}, u32[]{:S(2)}) %collective-permute-start.22) | collective-permute-done | bytes 65568 | tf_op jit(solution)/shard_map/ppermute | solution.py:176
  138.7 4.7 %collective-permute-done.20.xhi = f32[4,1,64,128]{3,2,1,0:T(8,128)S(1)} collective-permute-done((f32[4,1,64,128]{3,2,1,0:T(8,128)S(1)}, f32[4,1,64,128]{3,2,1,0:T(8,128)S(1)}, u32[]{:S(2)}, u32[]{:S(2)}) %collective-permute-start.20) | collective-permute-done | bytes 131104 | tf_op jit(solution)/shard_map/ppermute | solution.py:228
  143.5 6.2 %collective-permute-start.27 = (f32[4,1,64,128]{3,2,1,0:T(8,128)S(1)}, f32[4,1,64,128]{3,2,1,0:T(8,128)S(1)}, u32[]{:S(2)}, u32[]{:S(2)}) collective-permute-start(f32[4,1,64,128]{3,2,1,0:T(8,128)S(1)} %get-tuple-element.66), channel_id=1, source_target_pairs={{0,4},{4,8},{8,12},{12,16},{16,20},{20,24},{24,28},{1,5},{5,9},{9,... | collective-permute-start | bytes 393224 | tf_op jit(solution)/shard_map/ppermute | solution.py:228
  154.3 7.3 %step2_1.1 = (f32[4,32,64,128]{3,2,1,0:T(8,128)S(1)}, f32[32,64,128]{2,1,0:T(8,128)}, f32[32,64,128]{2,1,0:T(8,128)S(1)}, f32[4,32,1,128]{3,2,1,0:T(1,128)S(1)},...) custom-call(f32[4,32,64,128]{3,2,1,0:T(8,128)S(1)} %get-tuple-element.49.c.xhi, f32[4,64,64,128]{3,2,1,0:T(8,128)} %k.19, ...), custom_call_target="tpu_custom_call" | custom-call | flops 14680064 | bytes 12582912 | tf_op jit(solution)/shard_map/step2_1/pallas_call | solution.py:200
  167.0 7.3 %step2_0.1 = (f32[4,32,64,128]{3,2,1,0:T(8,128)S(1)}, f32[32,64,128]{2,1,0:T(8,128)}, f32[32,64,128]{2,1,0:T(8,128)}, f32[4,32,1,128]{3,2,1,0:T(1,128)S(1)}, f32...) custom-call(f32[4,32,64,128]{3,2,1,0:T(8,128)S(1)} %copy-done.11, f32[4,64,64,128]{3,2,1,0:T(8,128)} %k.19, ...), custom_call_target="tpu_custom_call" | custom-call | flops 14680064 | bytes 12582912 | tf_op jit(solution)/shard_map/step2_0/pallas_call | solution.py:200
  176.3 3.9 %collective-permute-start.36 = (f32[4,32,1,128]{3,2,1,0:T(1,128)S(1)}, f32[4,32,1,128]{3,2,1,0:T(1,128)S(1)}, u32[]{:S(2)}, u32[]{:S(2)}) collective-permute-start(f32[4,32,1,128]{3,2,1,0:T(1,128)S(1)} %get-tuple-element.76), channel_id=1, source_target_pairs={{0,1},{1,2},{2,3},{4,5},{5,6},{6,7},{8,9},{9,10},{10,11},{12,13},{... | collective-permute-start | bytes 196616 | tf_op jit(solution)/shard_map/ppermute | solution.py:176
  189.0 4.3 %collective-permute-start.23 = (f32[32,64,128]{2,1,0:T(8,128)S(1)}, f32[32,64,128]{2,1,0:T(8,128)S(1)}, u32[]{:S(2)}, u32[]{:S(2)}) collective-permute-start(f32[32,64,128]{2,1,0:T(8,128)S(1)} %get-tuple-element.62), channel_id=1, source_target_pairs={{0,32},{32,64},{64,96},{1,33},{33,65},{65,97},{2,34},{34,66},{66,9... | collective-permute-start | bytes 3145736 | tf_op jit(solution)/shard_map/ppermute | solution.py:173
  200.8 6.9 %total_0.1 = f32[32,64,128]{2,1,0:T(8,128)} custom-call(s32[1]{0:T(128)} %bitcast.place, f32[4,32,64,128]{3,2,1,0:T(8,128)S(1)} %copy-done.4, f32[4,64,64,128]{3,2,1,0:T(8,128)} %k.19, f32[4,1,64,128]{3,2,1,0:T(8,128)S(1)} %collective-permute-done.35.xlo, f32[4,32,64,128]{3,2,1,0:T(8,128)S(1)} %copy-done.1, ...), custom_call_target="tpu_custom_call" | custom-call | flops 14680064 | bytes 12582912 | tf_op jit(solution)/shard_map/total_0/pallas_call | solution.py:234
  212.4 6.9 %total_1.1 = f32[32,64,128]{2,1,0:T(8,128)} custom-call(s32[1]{0:T(128)} %bitcast.place, f32[4,32,64,128]{3,2,1,0:T(8,128)S(1)} %copy-done.1, f32[4,64,64,128]{3,2,1,0:T(8,128)} %k.19, f32[4,32,64,128]{3,2,1,0:T(8,128)S(1)} %copy-done.4, f32[4,1,64,128]{3,2,1,0:T(8,128)S(1)} %collective-permute-done.30.xhi, ...), custom_call_target="tpu_custom_call" | custom-call | flops 14680064 | bytes 12582912 | tf_op jit(solution)/shard_map/total_1/pallas_call | solution.py:234
  222.8 14.6 %collective-permute-done.33.ylo = f32[32,64,128]{2,1,0:T(8,128)S(1)} collective-permute-done((f32[32,64,128]{2,1,0:T(8,128)}, f32[32,64,128]{2,1,0:T(8,128)S(1)}, u32[]{:S(2)}, u32[]{:S(2)}) %collective-permute-start.33) | collective-permute-done | bytes 1048608 | tf_op jit(solution)/shard_map/ppermute | solution.py:173
  238.4 4.1 %collective-permute-start.41 = (f32[32,64,128]{2,1,0:T(8,128)}, f32[32,64,128]{2,1,0:T(8,128)S(1)}, u32[]{:S(2)}, u32[]{:S(2)}) collective-permute-start(f32[32,64,128]{2,1,0:T(8,128)} %total_0.1), channel_id=1, source_target_pairs={{0,32},{32,64},{64,96},{1,33},{33,65},{65,97},{2,34},{34,66},{66,9... | collective-permute-start | bytes 3145736 | tf_op jit(solution)/shard_map/ppermute | solution.py:245
  242.4 15.2 %collective-permute-done.42.two = f32[32,64,128]{2,1,0:T(8,128)S(1)} collective-permute-done((f32[32,64,128]{2,1,0:T(8,128)}, f32[32,64,128]{2,1,0:T(8,128)S(1)}, u32[]{:S(2)}, u32[]{:S(2)}) %collective-permute-start.42) | collective-permute-done | bytes 1048608 | tf_op jit(solution)/shard_map/ppermute | solution.py:244
  261.4 18.8 %collective-permute-done.39.two = f32[32,64,128]{2,1,0:T(8,128)S(1)} collective-permute-done((f32[32,64,128]{2,1,0:T(8,128)}, f32[32,64,128]{2,1,0:T(8,128)S(1)}, u32[]{:S(2)}, u32[]{:S(2)}) %collective-permute-start.39) | collective-permute-done | bytes 1048608 | tf_op jit(solution)/shard_map/ppermute | solution.py:244
  285.0 7.5 %last_0.1 = (f32[4,64,64,128]{3,2,1,0:T(8,128)}, f32[4,32,64,128]{3,2,1,0:T(8,128)S(1)}) custom-call(s32[1]{0:T(128)} %bitcast.place, f32[4,32,64,128]{3,2,1,0:T(8,128)S(1)} %copy-done.5, f32[4,64,64,128]{3,2,1,0:T(8,128)} %k.19, f32[32,64,128]{2,1,0:T(8,128)S(1)} %copy-done.13, f32[32,64,128]{2,1,0:T(8,128)S(1)} %copy-done.15, ...), custom_call_target="tpu_custom_call" | custom-call | flops 18874368 | bytes 12582912 | tf_op jit(solution)/shard_map/last_0/pallas_call | solution.py:260
  292.5 9.0 %collective-permute-done.24.yhi = f32[32,64,128]{2,1,0:T(8,128)S(1)} collective-permute-done((f32[32,64,128]{2,1,0:T(8,128)}, f32[32,64,128]{2,1,0:T(8,128)S(1)}, u32[]{:S(2)}, u32[]{:S(2)}) %collective-permute-start.24) | collective-permute-done | bytes 1048608 | tf_op jit(solution)/shard_map/ppermute | solution.py:173
  301.5 7.5 %last_1.1 = (f32[4,64,64,128]{3,2,1,0:T(8,128)}, f32[4,32,64,128]{3,2,1,0:T(8,128)S(1)}) custom-call(s32[1]{0:T(128)} %bitcast.place, f32[4,32,64,128]{3,2,1,0:T(8,128)S(1)} %copy-done.2, f32[4,64,64,128]{3,2,1,0:T(8,128)} %k.19, f32[32,64,128]{2,1,0:T(8,128)S(1)} %collective-permute-done.23.ylo, ...), custom_call_target="tpu_custom_call", output_to_operand_aliasing={{0}: (9, {})} | custom-call | flops 18874368 | bytes 12582912 | tf_op jit(solution)/shard_map/last_1/pallas_call | solution.py:260
  312.9 6.0 %add_1.1 = f32[4,64,64,128]{3,2,1,0:T(8,128)} custom-call(s32[1]{0:T(128)} %bitcast.place, f32[4,32,64,128]{3,2,1,0:T(8,128)S(1)} %get-tuple-element.79.sums, f32[32,64,128]{2,1,0:T(8,128)S(1)} %collective-permute-done.38.one, f32[32,64,128]{2,1,0:T(8,128)S(1)} %collective-permute-done.39.two, ...), custom_call_target="tpu_custom_call", output_to_operand_aliasing={{}: (5, {})} | custom-call | flops 3145728 | bytes 12582912 | tf_op jit(solution)/shard_map/add_1/pallas_call | solution.py:286
  (105 shorter events, 101.8 us)
Async XLA Ops:
  3.4 35.9 %collective-permute-start = (f32[32,64,128]{2,1,0:T(8,128)S(1)}, f32[32,64,128]{2,1,0:T(8,128)S(1)}, u32[]{:S(2)}, u32[]{:S(2)}) collective-permute-start(f32[32,64,128]{2,1,0:T(8,128)S(1)} %get-tuple-element.87), channel_id=1, source_target_pairs={{0,32},{32,64},{64,96},{1,33},{33,65},{65,97},{2,34},{34,66},{66,9... | collective-permute-start | bytes 3145736 | tf_op jit(solution)/shard_map/ppermute | solution.py:173
  7.8 31.5 %collective-permute-start.1 = (f32[32,64,128]{2,1,0:T(8,128)S(1)}, f32[32,64,128]{2,1,0:T(8,128)S(1)}, u32[]{:S(2)}, u32[]{:S(2)}) collective-permute-start(f32[32,64,128]{2,1,0:T(8,128)S(1)} %get-tuple-element.86), channel_id=1, source_target_pairs={{32,0},{64,32},{96,64},{33,1},{65,33},{97,65},{34,2},{66,34},{98,6... | collective-permute-start | bytes 3145736 | tf_op jit(solution)/shard_map/ppermute | solution.py:173
  9.1 43.4 %collective-permute-start.7 = (f32[32,64,128]{2,1,0:T(8,128)S(1)}, f32[32,64,128]{2,1,0:T(8,128)S(1)}, u32[]{:S(2)}, u32[]{:S(2)}) collective-permute-start(f32[32,64,128]{2,1,0:T(8,128)S(1)} %get-tuple-element.85), channel_id=1, source_target_pairs={{0,32},{32,64},{64,96},{1,33},{33,65},{65,97},{2,34},{34,66},{66,9... | collective-permute-start | bytes 3145736 | tf_op jit(solution)/shard_map/ppermute | solution.py:173
  13.3 42.9 %collective-permute-start.8 = (f32[32,64,128]{2,1,0:T(8,128)S(1)}, f32[32,64,128]{2,1,0:T(8,128)S(1)}, u32[]{:S(2)}, u32[]{:S(2)}) collective-permute-start(f32[32,64,128]{2,1,0:T(8,128)S(1)} %get-tuple-element.84), channel_id=1, source_target_pairs={{32,0},{64,32},{96,64},{33,1},{65,33},{97,65},{34,2},{66,34},{98,6... | collective-permute-start | bytes 3145736 | tf_op jit(solution)/shard_map/ppermute | solution.py:173
  36.2 16.3 %collective-permute-start.9 = (f32[4,1,64,128]{3,2,1,0:T(8,128)S(1)}, f32[4,1,64,128]{3,2,1,0:T(8,128)S(1)}, u32[]{:S(2)}, u32[]{:S(2)}) collective-permute-start(f32[4,1,64,128]{3,2,1,0:T(8,128)S(1)} %get-tuple-element.82), channel_id=1, source_target_pairs={{0,4},{4,8},{8,12},{12,16},{16,20},{20,24},{24,28},{1,5},{5,9},{9,... | collective-permute-start | bytes 393224 | tf_op jit(solution)/shard_map/ppermute | solution.py:181
  46.9 46.9 %collective-permute-start.5 = (f32[32,64,128]{2,1,0:T(8,128)S(1)}, f32[32,64,128]{2,1,0:T(8,128)S(1)}, u32[]{:S(2)}, u32[]{:S(2)}) collective-permute-start(f32[32,64,128]{2,1,0:T(8,128)S(1)} %get-tuple-element.43), channel_id=1, source_target_pairs={{0,32},{32,64},{64,96},{1,33},{33,65},{65,97},{2,34},{34,66},{66,9... | collective-permute-start | bytes 3145736 | tf_op jit(solution)/shard_map/ppermute | solution.py:173
  51.2 45.3 %collective-permute-start.6 = (f32[32,64,128]{2,1,0:T(8,128)S(1)}, f32[32,64,128]{2,1,0:T(8,128)S(1)}, u32[]{:S(2)}, u32[]{:S(2)}) collective-permute-start(f32[32,64,128]{2,1,0:T(8,128)S(1)} %get-tuple-element.44), channel_id=1, source_target_pairs={{32,0},{64,32},{96,64},{33,1},{65,33},{97,65},{34,2},{66,34},{98,6... | collective-permute-start | bytes 3145736 | tf_op jit(solution)/shard_map/ppermute | solution.py:173
  65.7 45.9 %collective-permute-start.15 = (f32[32,64,128]{2,1,0:T(8,128)S(1)}, f32[32,64,128]{2,1,0:T(8,128)S(1)}, u32[]{:S(2)}, u32[]{:S(2)}) collective-permute-start(f32[32,64,128]{2,1,0:T(8,128)S(1)} %get-tuple-element.52), channel_id=1, source_target_pairs={{0,32},{32,64},{64,96},{1,33},{33,65},{65,97},{2,34},{34,66},{66,9... | collective-permute-start | bytes 3145736 | tf_op jit(solution)/shard_map/ppermute | solution.py:173
  69.0 42.7 %collective-permute-start.16 = (f32[32,64,128]{2,1,0:T(8,128)S(1)}, f32[32,64,128]{2,1,0:T(8,128)S(1)}, u32[]{:S(2)}, u32[]{:S(2)}) collective-permute-start(f32[32,64,128]{2,1,0:T(8,128)S(1)} %get-tuple-element.53), channel_id=1, source_target_pairs={{32,0},{64,32},{96,64},{33,1},{65,33},{97,65},{34,2},{66,34},{98,6... | collective-permute-start | bytes 3145736 | tf_op jit(solution)/shard_map/ppermute | solution.py:173
  90.7 20.9 %collective-permute-start.17 = (f32[4,1,64,128]{3,2,1,0:T(8,128)S(1)}, f32[4,1,64,128]{3,2,1,0:T(8,128)S(1)}, u32[]{:S(2)}, u32[]{:S(2)}) collective-permute-start(f32[4,1,64,128]{3,2,1,0:T(8,128)S(1)} %get-tuple-element.54), channel_id=1, source_target_pairs={{0,4},{4,8},{8,12},{12,16},{16,20},{20,24},{24,28},{1,5},{5,9},{9,... | collective-permute-start | bytes 393224 | tf_op jit(solution)/shard_map/ppermute | solution.py:228
  96.5 13.8 %collective-permute-start.19 = (f32[4,32,1,128]{3,2,1,0:T(1,128)S(1)}, f32[4,32,1,128]{3,2,1,0:T(1,128)S(1)}, u32[]{:S(2)}, u32[]{:S(2)}) collective-permute-start(f32[4,32,1,128]{3,2,1,0:T(1,128)S(1)} %get-tuple-element.56), channel_id=1, source_target_pairs={{1,0},{2,1},{3,2},{5,4},{6,5},{7,6},{9,8},{10,9},{11,10},{13,12},{... | collective-permute-start | bytes 196616 | tf_op jit(solution)/shard_map/ppermute | solution.py:176
  105.9 43.7 %collective-permute-start.13 = (f32[32,64,128]{2,1,0:T(8,128)}, f32[32,64,128]{2,1,0:T(8,128)S(1)}, u32[]{:S(2)}, u32[]{:S(2)}) collective-permute-start(f32[32,64,128]{2,1,0:T(8,128)} %get-tuple-element.50), channel_id=1, source_target_pairs={{0,32},{32,64},{64,96},{1,33},{33,65},{65,97},{2,34},{34,66},{66,9... | collective-permute-start | bytes 3145736 | tf_op jit(solution)/shard_map/ppermute | solution.py:173
  110.3 42.0 %collective-permute-start.14 = (f32[32,64,128]{2,1,0:T(8,128)}, f32[32,64,128]{2,1,0:T(8,128)S(1)}, u32[]{:S(2)}, u32[]{:S(2)}) collective-permute-start(f32[32,64,128]{2,1,0:T(8,128)} %get-tuple-element.51), channel_id=1, source_target_pairs={{32,0},{64,32},{96,64},{33,1},{65,33},{97,65},{34,2},{66,34},{98,6... | collective-permute-start | bytes 3145736 | tf_op jit(solution)/shard_map/ppermute | solution.py:173
  119.8 47.1 %collective-permute-start.25 = (f32[32,64,128]{2,1,0:T(8,128)S(1)}, f32[32,64,128]{2,1,0:T(8,128)S(1)}, u32[]{:S(2)}, u32[]{:S(2)}) collective-permute-start(f32[32,64,128]{2,1,0:T(8,128)S(1)} %get-tuple-element.64), channel_id=1, source_target_pairs={{0,32},{32,64},{64,96},{1,33},{33,65},{65,97},{2,34},{34,66},{66,9... | collective-permute-start | bytes 3145736 | tf_op jit(solution)/shard_map/ppermute | solution.py:173
  123.9 43.1 %collective-permute-start.26 = (f32[32,64,128]{2,1,0:T(8,128)S(1)}, f32[32,64,128]{2,1,0:T(8,128)S(1)}, u32[]{:S(2)}, u32[]{:S(2)}) collective-permute-start(f32[32,64,128]{2,1,0:T(8,128)S(1)} %get-tuple-element.65), channel_id=1, source_target_pairs={{32,0},{64,32},{96,64},{33,1},{65,33},{97,65},{34,2},{66,34},{98,6... | collective-permute-start | bytes 3145736 | tf_op jit(solution)/shard_map/ppermute | solution.py:173
  143.5 23.5 %collective-permute-start.27 = (f32[4,1,64,128]{3,2,1,0:T(8,128)S(1)}, f32[4,1,64,128]{3,2,1,0:T(8,128)S(1)}, u32[]{:S(2)}, u32[]{:S(2)}) collective-permute-start(f32[4,1,64,128]{3,2,1,0:T(8,128)S(1)} %get-tuple-element.66), channel_id=1, source_target_pairs={{0,4},{4,8},{8,12},{12,16},{16,20},{20,24},{24,28},{1,5},{5,9},{9,... | collective-permute-start | bytes 393224 | tf_op jit(solution)/shard_map/ppermute | solution.py:228
  149.7 13.8 %collective-permute-start.28 = (f32[4,32,1,128]{3,2,1,0:T(1,128)S(1)}, f32[4,32,1,128]{3,2,1,0:T(1,128)S(1)}, u32[]{:S(2)}, u32[]{:S(2)}) collective-permute-start(f32[4,32,1,128]{3,2,1,0:T(1,128)S(1)} %get-tuple-element.67), channel_id=1, source_target_pairs={{0,1},{1,2},{2,3},{4,5},{5,6},{6,7},{8,9},{9,10},{10,11},{12,13},{... | collective-permute-start | bytes 196616 | tf_op jit(solution)/shard_map/ppermute | solution.py:176
  152.3 14.6 %collective-permute-start.29 = (f32[4,32,1,128]{3,2,1,0:T(1,128)S(1)}, f32[4,32,1,128]{3,2,1,0:T(1,128)S(1)}, u32[]{:S(2)}, u32[]{:S(2)}) collective-permute-start(f32[4,32,1,128]{3,2,1,0:T(1,128)S(1)} %get-tuple-element.68), channel_id=1, source_target_pairs={{1,0},{2,1},{3,2},{5,4},{6,5},{7,6},{9,8},{10,9},{11,10},{13,12},{... | collective-permute-start | bytes 196616 | tf_op jit(solution)/shard_map/ppermute | solution.py:176
  163.5 29.8 %collective-permute-start.35 = (f32[4,1,64,128]{3,2,1,0:T(8,128)S(1)}, f32[4,1,64,128]{3,2,1,0:T(8,128)S(1)}, u32[]{:S(2)}, u32[]{:S(2)}) collective-permute-start(f32[4,1,64,128]{3,2,1,0:T(8,128)S(1)} %get-tuple-element.75), channel_id=1, source_target_pairs={{0,4},{4,8},{8,12},{12,16},{16,20},{20,24},{24,28},{1,5},{5,9},{9,... | collective-permute-start | bytes 393224 | tf_op jit(solution)/shard_map/ppermute | solution.py:228
  180.2 32.2 %collective-permute-start.30 = (f32[4,1,64,128]{3,2,1,0:T(8,128)S(1)}, f32[4,1,64,128]{3,2,1,0:T(8,128)S(1)}, u32[]{:S(2)}, u32[]{:S(2)}) collective-permute-start(f32[4,1,64,128]{3,2,1,0:T(8,128)S(1)} %get-tuple-element.70), channel_id=1, source_target_pairs={{4,0},{8,4},{12,8},{16,12},{20,16},{24,20},{28,24},{5,1},{9,5},{13... | collective-permute-start | bytes 393224 | tf_op jit(solution)/shard_map/ppermute | solution.py:228
  183.4 24.3 %collective-permute-start.31 = (f32[4,32,1,128]{3,2,1,0:T(1,128)S(1)}, f32[4,32,1,128]{3,2,1,0:T(1,128)S(1)}, u32[]{:S(2)}, u32[]{:S(2)}) collective-permute-start(f32[4,32,1,128]{3,2,1,0:T(1,128)S(1)} %get-tuple-element.71), channel_id=1, source_target_pairs={{0,1},{1,2},{2,3},{4,5},{5,6},{6,7},{8,9},{9,10},{10,11},{12,13},{... | collective-permute-start | bytes 196616 | tf_op jit(solution)/shard_map/ppermute | solution.py:176
  187.1 22.2 %collective-permute-start.32 = (f32[4,32,1,128]{3,2,1,0:T(1,128)S(1)}, f32[4,32,1,128]{3,2,1,0:T(1,128)S(1)}, u32[]{:S(2)}, u32[]{:S(2)}) collective-permute-start(f32[4,32,1,128]{3,2,1,0:T(1,128)S(1)} %get-tuple-element.72), channel_id=1, source_target_pairs={{1,0},{2,1},{3,2},{5,4},{6,5},{7,6},{9,8},{10,9},{11,10},{13,12},{... | collective-permute-start | bytes 196616 | tf_op jit(solution)/shard_map/ppermute | solution.py:176
  189.0 32.3 %collective-permute-start.23 = (f32[32,64,128]{2,1,0:T(8,128)S(1)}, f32[32,64,128]{2,1,0:T(8,128)S(1)}, u32[]{:S(2)}, u32[]{:S(2)}) collective-permute-start(f32[32,64,128]{2,1,0:T(8,128)S(1)} %get-tuple-element.62), channel_id=1, source_target_pairs={{0,32},{32,64},{64,96},{1,33},{33,65},{65,97},{2,34},{34,66},{66,9... | collective-permute-start | bytes 3145736 | tf_op jit(solution)/shard_map/ppermute | solution.py:173
  193.4 44.1 %collective-permute-start.33 = (f32[32,64,128]{2,1,0:T(8,128)}, f32[32,64,128]{2,1,0:T(8,128)S(1)}, u32[]{:S(2)}, u32[]{:S(2)}) collective-permute-start(f32[32,64,128]{2,1,0:T(8,128)} %get-tuple-element.73), channel_id=1, source_target_pairs={{0,32},{32,64},{64,96},{1,33},{33,65},{65,97},{2,34},{34,66},{66,9... | collective-permute-start | bytes 3145736 | tf_op jit(solution)/shard_map/ppermute | solution.py:173
  207.7 51.4 %collective-permute-start.34 = (f32[32,64,128]{2,1,0:T(8,128)}, f32[32,64,128]{2,1,0:T(8,128)S(1)}, u32[]{:S(2)}, u32[]{:S(2)}) collective-permute-start(f32[32,64,128]{2,1,0:T(8,128)} %get-tuple-element.74), channel_id=1, source_target_pairs={{32,0},{64,32},{96,64},{33,1},{65,33},{97,65},{34,2},{66,34},{98,6... | collective-permute-start | bytes 3145736 | tf_op jit(solution)/shard_map/ppermute | solution.py:173
  209.2 48.4 %collective-permute-start.42 = (f32[32,64,128]{2,1,0:T(8,128)}, f32[32,64,128]{2,1,0:T(8,128)S(1)}, u32[]{:S(2)}, u32[]{:S(2)}) collective-permute-start(f32[32,64,128]{2,1,0:T(8,128)} %total_0.1), channel_id=1, source_target_pairs={{0,96},{32,0},{1,97},{33,1},{2,98},{34,2},{3,99},{35,3},{4,100},{3... | collective-permute-start | bytes 3145736 | tf_op jit(solution)/shard_map/ppermute | solution.py:244
  219.3 60.8 %collective-permute-start.39 = (f32[32,64,128]{2,1,0:T(8,128)}, f32[32,64,128]{2,1,0:T(8,128)S(1)}, u32[]{:S(2)}, u32[]{:S(2)}) collective-permute-start(f32[32,64,128]{2,1,0:T(8,128)} %total_1.1), channel_id=1, source_target_pairs={{0,96},{32,0},{1,97},{33,1},{2,98},{34,2},{3,99},{35,3},{4,100},{3... | collective-permute-start | bytes 3145736 | tf_op jit(solution)/shard_map/ppermute | solution.py:244
  221.3 80.2 %collective-permute-start.24 = (f32[32,64,128]{2,1,0:T(8,128)}, f32[32,64,128]{2,1,0:T(8,128)S(1)}, u32[]{:S(2)}, u32[]{:S(2)}) collective-permute-start(f32[32,64,128]{2,1,0:T(8,128)} %get-tuple-element.63), channel_id=1, source_target_pairs={{32,0},{64,32},{96,64},{33,1},{65,33},{97,65},{34,2},{66,34},{98,6... | collective-permute-start | bytes 3145736 | tf_op jit(solution)/shard_map/ppermute | solution.py:173
  238.4 70.7 %collective-permute-start.41 = (f32[32,64,128]{2,1,0:T(8,128)}, f32[32,64,128]{2,1,0:T(8,128)S(1)}, u32[]{:S(2)}, u32[]{:S(2)}) collective-permute-start(f32[32,64,128]{2,1,0:T(8,128)} %total_0.1), channel_id=1, source_target_pairs={{0,32},{32,64},{64,96},{1,33},{33,65},{65,97},{2,34},{34,66},{66,9... | collective-permute-start | bytes 3145736 | tf_op jit(solution)/shard_map/ppermute | solution.py:245
  257.7 51.4 %collective-permute-start.43 = (f32[32,64,128]{2,1,0:T(8,128)S(1)}, f32[32,64,128]{2,1,0:T(8,128)S(1)}, u32[]{:S(2)}, u32[]{:S(2)}) collective-permute-start(f32[32,64,128]{2,1,0:T(8,128)S(1)} %collective-permute-done.42.two), channel_id=1, source_target_pairs={{96,64},{0,96},{97,65},{1,97},{98,66},{2,98},{99,67},{3,99},{100,6... | collective-permute-start | bytes 3145736 | tf_op jit(solution)/shard_map/ppermute | solution.py:246
  260.0 52.8 %collective-permute-start.38 = (f32[32,64,128]{2,1,0:T(8,128)}, f32[32,64,128]{2,1,0:T(8,128)S(1)}, u32[]{:S(2)}, u32[]{:S(2)}) collective-permute-start(f32[32,64,128]{2,1,0:T(8,128)} %total_1.1), channel_id=1, source_target_pairs={{0,32},{32,64},{64,96},{1,33},{33,65},{65,97},{2,34},{34,66},{66,9... | collective-permute-start | bytes 3145736 | tf_op jit(solution)/shard_map/ppermute | solution.py:245
  280.2 32.7 %collective-permute-start.40 = (f32[32,64,128]{2,1,0:T(8,128)S(1)}, f32[32,64,128]{2,1,0:T(8,128)}, u32[]{:S(2)}, u32[]{:S(2)}) collective-permute-start(f32[32,64,128]{2,1,0:T(8,128)S(1)} %collective-permute-done.39.two), channel_id=1, source_target_pairs={{96,64},{0,96},{97,65},{1,97},{98,66},{2,98},{99,67},{3,99},{100,6... | collective-permute-start | bytes 3145736 | tf_op jit(solution)/shard_map/ppermute | solution.py:246
  (28 other events, 387.4 us)

commit v2 on v1

v2 whole, which is shorter than its diff:
```python
import functools

import jax
import jax.numpy as jnp
from jax import lax
from jax.experimental import pallas as pl
from jax.experimental.pallas import tpu as pltpu
from jax.sharding import PartitionSpec as P


STEPS = 4
CHUNKS = 2
PLANES = 4
VMEM = 16 * 2**20


def stencil(refs, masked_low):
    c, before_x, after_x, k, ylo, yhi, xlo, xhi, zlo, zhi = refs
    rows, planes, zs, lanes = k.shape
    z = lax.broadcasted_iota(jnp.int32, (zs, lanes), 0)
    i, last = pl.program_id(0), pl.num_programs(0) - 1

    def plane(y, xx):
        mid = c[y, xx]
        left = c[y, xx - 1] if xx else jnp.where(i == 0, xlo[y, 0], before_x[y, 0])
        right = c[y, xx + 1] if xx < planes - 1 else jnp.where(i == last, xhi[y, 0], after_x[y, 0])
        down = jnp.where(z == 0, zlo[y, xx], pltpu.roll(mid, 1, 0))
        up = jnp.where(z == zs - 1, zhi[y, xx], pltpu.roll(mid, zs - 1, 0))
        if y > 0:
            before = c[y - 1, xx]
        elif ylo is None:
            before = masked_low * mid
        else:
            before = ylo[xx]
        if y < rows - 1:
            after = c[y + 1, xx]
        elif yhi is None:
            after = mid
        else:
            after = yhi[xx]
        around = ((before + after) + (left + right)) + (down + up)
        return mid * (0.6 - (0.2 * mid) * k[y, xx]) + 0.1 * around

    return plane


def step_kernel(c, cl, cr, k, ylo, yhi, xlo, xhi, zlo, zhi, out, row_lo, row_hi, zlo_out, zhi_out, edge, *, edge_x):
    i = pl.program_id(0)
    rows, planes, zs, _ = k.shape
    plane = stencil((c, cl, cr, k, ylo, yhi, xlo, xhi, zlo, zhi), None)
    for xx in range(planes):
        for y in range(rows):
            new = plane(y, xx)
            out[y, xx] = new
            zlo_out[y, xx] = new[0:1]
            zhi_out[y, xx] = new[zs - 1 : zs]
            if y == 0:
                row_lo[xx] = new
            if y == rows - 1:
                row_hi[xx] = new
            if edge_x is not None and edge_x % planes == xx:

                @pl.when(i == edge_x // planes)
                def _():
                    edge[y, 0] = new


def total_kernel(place, c, cl, cr, k, xlo, xhi, zlo, zhi, total):
    rows, planes, _, _ = k.shape
    inside = jnp.where(place[0] > 0, 1.0, 0.0).astype(jnp.float32)
    plane = stencil((c, cl, cr, k, None, None, xlo, xhi, zlo, zhi), inside)
    for xx in range(planes):
        value = plane(0, xx)
        for y in range(1, rows):
            value = value + plane(y, xx)
        total[xx] = value


def last_kernel(place, c, cl, cr, k, ylo, yhi, xlo, xhi, zlo, zhi, *rest):
    out, sums = rest[-2:]
    rows, planes, _, _ = k.shape
    inside = jnp.where(place[0] > 0, 0.1, 0.0).astype(jnp.float32)
    plane = stencil((c, cl, cr, k, ylo, yhi, xlo, xhi, zlo, zhi), None)
    for xx in range(planes):
        sofar = inside * c[0, xx] - 0.1 * ylo[xx]
        for y in range(rows):
            new = plane(y, xx)
            out[y, xx] = new
            sofar = sofar + new
            sums[y, xx] = sofar


def add_kernel(place, sums, one, two, three, *rest, scale):
    out = rest[-1]
    rows, planes, _, _ = sums.shape
    inside = jnp.where(place[0] > 0, 1.0, 0.0).astype(jnp.float32)
    for xx in range(planes):
        below = one[xx] + inside * two[xx] + three[xx]
        for y in range(rows):
            out[y, xx] = (sums[y, xx] + below) * scale


def in_hbm(array):
    return pltpu.with_memory_space_constraint(array, pltpu.HBM)


class Source:
    def __init__(self, array, start, length):
        self.array, self.start, self.length = in_hbm(array), start, length

    def plane(self, x):
        rows, _, zs, lanes = self.array.shape
        at = self.start + x
        return (self.array, pl.BlockSpec((rows, 1, zs, lanes), lambda i: (0, at, 0, 0)))

    def blocks(self, planes):
        rows, _, zs, lanes = self.array.shape
        at = self.start // planes
        return (self.array, pl.BlockSpec((rows, planes, zs, lanes), lambda i: (0, at + i, 0, 0)))

    def with_sides(self, planes):
        rows, _, zs, lanes = self.array.shape
        start, end = self.start, self.start + self.length - 1
        before = pl.BlockSpec((rows, 1, zs, lanes), lambda i: (0, jnp.maximum(start + i * planes - 1, start), 0, 0))
        after = pl.BlockSpec((rows, 1, zs, lanes), lambda i: (0, jnp.minimum(start + (i + 1) * planes, end), 0, 0))
        return [self.blocks(planes), (self.array, before), (self.array, after)]


def rows_spec(planes, zs, lanes):
    return pl.BlockSpec((planes, zs, lanes), lambda i: (i, 0, 0))


def edge_spec(rows, planes, lanes):
    return pl.BlockSpec((rows, planes, 1, lanes), lambda i: (0, i, 0, 0))


def cost(cells, per_cell):
    return pl.CostEstimate(flops=cells * per_cell, bytes_accessed=cells * 12, transcendentals=0)


SMEM = pl.BlockSpec(memory_space=pltpu.SMEM)
ANY = pl.BlockSpec(memory_space=pl.ANY)


def shifts(axis):
    count = lax.axis_size(axis)
    up = [(i, i + 1) for i in range(count - 1)]
    return up, [(b, a) for a, b in up]


def program(tracer, crowding):
    rows, xs, zs, lanes = tracer.shape
    n = CHUNKS
    size = xs // n
    planes = PLANES
    grid = (size // planes,)
    cells = rows * size * zs * lanes
    f32 = jnp.float32
    place = lax.axis_index("rows").astype(jnp.int32)
    row_up, row_down = shifts("rows")
    col_up, col_down = shifts("cols")
    slab_up, slab_down = shifts("slabs")
    params = pltpu.CompilerParams(dimension_semantics=("arbitrary",), vmem_limit_bytes=VMEM)
    row_block = rows_spec(planes, zs, lanes)
    edge_block = edge_spec(rows, planes, lanes)
    block = pl.BlockSpec((rows, planes, zs, lanes), lambda i: (0, i, 0, 0))
    side_block = pl.BlockSpec((rows, 1, zs, lanes), lambda i: (0, 0, 0, 0))
    row_shape = jax.ShapeDtypeStruct((size, zs, lanes), f32)
    edge_shape = jax.ShapeDtypeStruct((rows, size, 1, lanes), f32)
    full = pltpu.HBM(tracer.shape, f32)

    def call(kernel, inputs, out_specs, out_shape, per_cell, alias=None):
        extra, aliases = [], {}
        if alias is not None:
            extra, aliases = [(alias, ANY)], {len(inputs): 0}
        arrays, specs = zip(*inputs, *extra)
        return pl.pallas_call(
            kernel,
            grid=grid,
            in_specs=list(specs),
            out_specs=out_specs,
            out_shape=out_shape,
            input_output_aliases=aliases,
            compiler_params=params,
            cost_estimate=cost(cells, per_cell),
        )(*arrays)

    def send_rows(lo, hi):
        return (lax.ppermute(hi, "rows", row_up), lax.ppermute(lo, "rows", row_down))

    def send_z(lo, hi):
        return (lax.ppermute(hi, "slabs", slab_up), lax.ppermute(lo, "slabs", slab_down))

    here = (place.reshape(1), SMEM)
    field = [Source(tracer, j * size, size) for j in range(n)]
    crowd = [Source(crowding, j * size, size) for j in range(n)]

    halo_y = []
    source = tracer
    for j in range(n):
        lo, hi = (source[r, j * size : (j + 1) * size] for r in (0, rows - 1))
        lo, hi, source = lax.optimization_barrier((lo, hi, source))
        halo_y.append(send_rows(lo, hi))
    halo_x = (lax.ppermute(tracer[:, xs - 1 : xs], "cols", col_up), lax.ppermute(tracer[:, 0:1], "cols", col_down))
    z_all = send_z(tracer[:, :, 0:1], tracer[:, :, zs - 1 : zs])
    halo_z = [tuple(side[:, j * size : (j + 1) * size] for side in z_all) for j in range(n)]

    def sides(j):
        low = field[j - 1].plane(size - 1) if j else (halo_x[0], side_block)
        high = field[j + 1].plane(0) if j < n - 1 else (halo_x[1], side_block)
        return [low, high, *((side, edge_block) for side in halo_z[j])]

    def near(j):
        return [*field[j].with_sides(planes), crowd[j].blocks(planes)]

    for _ in range(STEPS - 1):
        made, next_y, next_z, edges = [], [], [], {}
        for j in range(n):
            edge_x = {0: 0, n - 1: size - 1}.get(j)
            out, lo, hi, zlo, zhi, edge = call(
                functools.partial(step_kernel, edge_x=edge_x),
                [*near(j), *((side, row_block) for side in halo_y[j]), *sides(j)],
                [block, row_block, row_block, edge_block, edge_block, side_block],
                [
                    pltpu.HBM((rows, size, zs, lanes), f32),
                    row_shape,
                    row_shape,
                    edge_shape,
                    edge_shape,
                    jax.ShapeDtypeStruct((rows, 1, zs, lanes), f32),
                ],
                14,
            )
            made.append(Source(out, 0, size))
            next_y.append(send_rows(lo, hi))
            next_z.append(send_z(zlo, zhi))
            edges[j] = edge
        halo_x = (lax.ppermute(edges[n - 1], "cols", col_up), lax.ppermute(edges[0], "cols", col_down))
        field, halo_y, halo_z = made, next_y, next_z

    total = [call(total_kernel, [here, *near(j), *sides(j)], row_block, row_shape, 14) for j in range(n)]
    one, two, three = [None] * n, [None] * n, [None] * n
    two[1] = lax.ppermute(total[1], "rows", [(0, 3), (1, 0)])
    one[0] = lax.ppermute(total[0], "rows", [(0, 1), (1, 2)])
    two[0] = lax.ppermute(total[0], "rows", [(0, 3)])
    passed = jnp.where(place == 2, total[0] + one[0], two[0])
    three[0] = lax.ppermute(passed, "rows", [(2, 3), (3, 2)])
    one[1] = lax.ppermute(total[1], "rows", row_up)
    three[1] = lax.ppermute(two[1], "rows", [(3, 2), (0, 3)])

    end, column = None, None
    sums = []
    for j in range(n):
        end, partial = call(
            last_kernel,
            [here, *near(j), *((side, row_block) for side in halo_y[j]), *sides(j)],
            [pl.BlockSpec((rows, planes, zs, lanes), lambda i, j=j: (0, j * grid[0] + i, 0, 0)), block],
            [full, pltpu.HBM((rows, size, zs, lanes), f32)],
            18,
            alias=end,
        )
        sums.append(partial)
    for j in range(n):
        column = call(
            functools.partial(add_kernel, scale=1.0 / (rows * lax.axis_size("rows"))),
            [here, (in_hbm(sums[j]), block), (one[j], row_block), (two[j], row_block), (three[j], row_block)],
            pl.BlockSpec((rows, planes, zs, lanes), lambda i, j=j: (0, j * grid[0] + i, 0, 0)),
            full,
            3,
            alias=column,
        )
    return column, end


def solution(mesh):
    spec = P("rows", "cols", "slabs", None)
    return jax.shard_map(program, mesh=mesh, in_specs=(spec, spec), out_specs=(spec, spec), check_vma=False)
```

time: 324 us -> 313 us (0.966)
  the two profiles are of different devices: /device:TPU:1 before, /device:TPU:69 now
where the time goes in v2:
time: 313 us; the launch traced here: 309 us
  starting transfers between devices  123 us (39%)
  Pallas kernels  104 us (33%)
  waiting for transfers between devices  73.7 us (24%)
  local copies, waits for them, and re-layouts  7 us (2%)
    pallas_call x12, Pallas kernels, call(): pl.pallas_call(kernel, grid=grid, in_specs=list(specs), out_specs=out_spe...  104 us
    ppermute x7, starting transfers between devices, send_z(): lax.ppermute(hi, 'slabs', slab_up)  25.1 us
    ppermute x8, starting transfers between devices, send_rows(): lax.ppermute(lo, 'rows', row_down)  22.1 us
    ppermute x8, waiting for transfers between devices, send_rows(): lax.ppermute(hi, 'rows', row_up)  21.5 us
    ppermute x8, starting transfers between devices, send_rows(): lax.ppermute(hi, 'rows', row_up)  21.1 us
    ppermute x7, waiting for transfers between devices, send_z(): lax.ppermute(lo, 'slabs', slab_down)  19.9 us
    ppermute x3, starting transfers between devices, program(): lax.ppermute(edges[n - 1], 'cols', col_up)  14.3 us
    ppermute x7, starting transfers between devices, send_z(): lax.ppermute(lo, 'slabs', slab_down)  13.7 us
  transfers between devices with their start and end apart: 44, of which 16 were waited for; matrix products, arithmetic and copies ran while one was open for 1% of the time, Pallas kernels for 29%

profile of v2, /device:TPU:69, one launch (start us, length us, event | category | flops | bytes accessed | tf_op | source)
XLA Modules:
  0.0 309.2 jit_solution(9887776289374611182)
XLA Ops:
  16.6 4.9 %collective-permute-start.3 = (f32[4,64,1,128]{3,2,1,0:T(1,128)S(1)}, f32[4,64,1,128]{3,2,1,0:T(1,128)S(1)}, u32[]{:S(2)}, u32[]{:S(2)}) collective-permute-start(f32[4,64,1,128]{3,2,1,0:T(1,128)S(1)} %get-tuple-element.95), channel_id=1, source_target_pairs={{0,1},{1,2},{2,3},{4,5},{5,6},{6,7},{8,9},{9,10},{10,11},{12,13},{... | collective-permute-start | bytes 393224 | tf_op jit(solution)/shard_map/ppermute | solution.py:192
  25.3 5.3 %collective-permute-done.4 = f32[4,64,1,128]{3,2,1,0:T(1,128)S(1)} collective-permute-done((f32[4,64,1,128]{3,2,1,0:T(1,128)S(1)}, f32[4,64,1,128]{3,2,1,0:T(1,128)S(1)}, u32[]{:S(2)}, u32[]{:S(2)}) %collective-permute-start.4) | collective-permute-done | bytes 131104 | tf_op jit(solution)/shard_map/ppermute | solution.py:192
  32.8 3.8 %collective-permute-done.2.xhi = f32[4,1,64,128]{3,2,1,0:T(8,128)S(1)} collective-permute-done((f32[4,1,64,128]{3,2,1,0:T(8,128)S(1)}, f32[4,1,64,128]{3,2,1,0:T(8,128)S(1)}, u32[]{:S(2)}, u32[]{:S(2)}) %collective-permute-start.2) | collective-permute-done | bytes 131104 | tf_op jit(solution)/shard_map/ppermute | solution.py:204
  36.6 6.1 %collective-permute-start.9 = (f32[4,1,64,128]{3,2,1,0:T(8,128)S(1)}, f32[4,1,64,128]{3,2,1,0:T(8,128)S(1)}, u32[]{:S(2)}, u32[]{:S(2)}) collective-permute-start(f32[4,1,64,128]{3,2,1,0:T(8,128)S(1)} %get-tuple-element.92), channel_id=1, source_target_pairs={{0,4},{4,8},{8,12},{12,16},{16,20},{20,24},{24,28},{1,5},{5,9},{9,... | collective-permute-start | bytes 393224 | tf_op jit(solution)/shard_map/ppermute | solution.py:204
  42.8 8.9 %shard_map.41 = (f32[4,32,64,128]{3,2,1,0:T(8,128)}, f32[32,64,128]{2,1,0:T(8,128)S(1)}, f32[32,64,128]{2,1,0:T(8,128)S(1)}, f32[4,32,1,128]{3,2,1,0:T(1,128)S(1...) custom-call(f32[4,64,64,128]{3,2,1,0:T(8,128)} %xhi.1, f32[4,64,64,128]{3,2,1,0:T(8,128)} %xhi.1, ...), custom_call_target="tpu_custom_call" | custom-call | flops 14680064 | bytes 12582912 | tf_op jit(solution)/shard_map/pallas_call | solution.py:177
  57.0 8.9 %shard_map.42 = (f32[4,32,64,128]{3,2,1,0:T(8,128)}, f32[32,64,128]{2,1,0:T(8,128)S(1)}, f32[32,64,128]{2,1,0:T(8,128)S(1)}, f32[4,32,1,128]{3,2,1,0:T(1,128)S(1...) custom-call(f32[4,64,64,128]{3,2,1,0:T(8,128)} %xhi.1, f32[4,64,64,128]{3,2,1,0:T(8,128)} %xhi.1, ...), custom_call_target="tpu_custom_call" | custom-call | flops 14680064 | bytes 12582912 | tf_op jit(solution)/shard_map/pallas_call | solution.py:177
  71.2 4.4 %collective-permute-start.11 = (f32[4,32,1,128]{3,2,1,0:T(1,128)S(1)}, f32[4,32,1,128]{3,2,1,0:T(1,128)S(1)}, u32[]{:S(2)}, u32[]{:S(2)}) collective-permute-start(f32[4,32,1,128]{3,2,1,0:T(1,128)S(1)} %get-tuple-element.57), channel_id=1, source_target_pairs={{0,1},{1,2},{2,3},{4,5},{5,6},{6,7},{8,9},{9,10},{10,11},{12,13},{... | collective-permute-start | bytes 196616 | tf_op jit(solution)/shard_map/ppermute | solution.py:192
  78.9 4.6 %collective-permute-done.12.zhi = f32[4,32,1,128]{3,2,1,0:T(1,128)S(1)} collective-permute-done((f32[4,32,1,128]{3,2,1,0:T(1,128)S(1)}, f32[4,32,1,128]{3,2,1,0:T(1,128)S(1)}, u32[]{:S(2)}, u32[]{:S(2)}) %collective-permute-start.12) | collective-permute-done | bytes 65568 | tf_op jit(solution)/shard_map/ppermute | solution.py:192
  92.2 7.0 %collective-permute-start.17 = (f32[4,1,64,128]{3,2,1,0:T(8,128)S(1)}, f32[4,1,64,128]{3,2,1,0:T(8,128)S(1)}, u32[]{:S(2)}, u32[]{:S(2)}) collective-permute-start(f32[4,1,64,128]{3,2,1,0:T(8,128)S(1)} %get-tuple-element.64), channel_id=1, source_target_pairs={{0,4},{4,8},{8,12},{12,16},{16,20},{20,24},{24,28},{1,5},{5,9},{9,... | collective-permute-start | bytes 393224 | tf_op jit(solution)/shard_map/ppermute | solution.py:238
  101.2 8.9 %shard_map.43 = (f32[4,32,64,128]{3,2,1,0:T(8,128)}, f32[32,64,128]{2,1,0:T(8,128)S(1)}, f32[32,64,128]{2,1,0:T(8,128)S(1)}, f32[4,32,1,128]{3,2,1,0:T(1,128)S(1...) custom-call(f32[4,32,64,128]{3,2,1,0:T(8,128)} %get-tuple-element.50.c.cl.cr.xhi, ...), custom_call_target="tpu_custom_call" | custom-call | flops 14680064 | bytes 12582912 | tf_op jit(solution)/shard_map/pallas_call | solution.py:177
  115.4 8.9 %shard_map.44 = (f32[4,32,64,128]{3,2,1,0:T(8,128)}, f32[32,64,128]{2,1,0:T(8,128)S(1)}, f32[32,64,128]{2,1,0:T(8,128)S(1)}, f32[4,32,1,128]{3,2,1,0:T(1,128)S(1...) custom-call(f32[4,32,64,128]{3,2,1,0:T(8,128)} %get-tuple-element.55.xlo.c.cl.cr, ...), custom_call_target="tpu_custom_call" | custom-call | flops 14680064 | bytes 12582912 | tf_op jit(solution)/shard_map/pallas_call | solution.py:177
  129.6 4.8 %collective-permute-start.21 = (f32[4,32,1,128]{3,2,1,0:T(1,128)S(1)}, f32[4,32,1,128]{3,2,1,0:T(1,128)S(1)}, u32[]{:S(2)}, u32[]{:S(2)}) collective-permute-start(f32[4,32,1,128]{3,2,1,0:T(1,128)S(1)} %get-tuple-element.69), channel_id=1, source_target_pairs={{0,1},{1,2},{2,3},{4,5},{5,6},{6,7},{8,9},{9,10},{10,11},{12,13},{... | collective-permute-start | bytes 196616 | tf_op jit(solution)/shard_map/ppermute | solution.py:192
  137.6 4.6 %collective-permute-done.22.zhi = f32[4,32,1,128]{3,2,1,0:T(1,128)S(1)} collective-permute-done((f32[4,32,1,128]{3,2,1,0:T(1,128)S(1)}, f32[4,32,1,128]{3,2,1,0:T(1,128)S(1)}, u32[]{:S(2)}, u32[]{:S(2)}) %collective-permute-start.22) | collective-permute-done | bytes 65568 | tf_op jit(solution)/shard_map/ppermute | solution.py:192
  144.1 4.1 %collective-permute-done.20.xhi = f32[4,1,64,128]{3,2,1,0:T(8,128)S(1)} collective-permute-done((f32[4,1,64,128]{3,2,1,0:T(8,128)S(1)}, f32[4,1,64,128]{3,2,1,0:T(8,128)S(1)}, u32[]{:S(2)}, u32[]{:S(2)}) %collective-permute-start.20) | collective-permute-done | bytes 131104 | tf_op jit(solution)/shard_map/ppermute | solution.py:238
  148.2 5.3 %collective-permute-start.27 = (f32[4,1,64,128]{3,2,1,0:T(8,128)S(1)}, f32[4,1,64,128]{3,2,1,0:T(8,128)S(1)}, u32[]{:S(2)}, u32[]{:S(2)}) collective-permute-start(f32[4,1,64,128]{3,2,1,0:T(8,128)S(1)} %get-tuple-element.76), channel_id=1, source_target_pairs={{0,4},{4,8},{8,12},{12,16},{16,20},{20,24},{24,28},{1,5},{5,9},{9,... | collective-permute-start | bytes 393224 | tf_op jit(solution)/shard_map/ppermute | solution.py:238
  158.4 8.9 %shard_map.45 = (f32[4,32,64,128]{3,2,1,0:T(8,128)}, f32[32,64,128]{2,1,0:T(8,128)S(1)}, f32[32,64,128]{2,1,0:T(8,128)S(1)}, f32[4,32,1,128]{3,2,1,0:T(1,128)S(1...) custom-call(f32[4,32,64,128]{3,2,1,0:T(8,128)} %get-tuple-element.59.c.cl.cr.xhi, ...), custom_call_target="tpu_custom_call" | custom-call | flops 14680064 | bytes 12582912 | tf_op jit(solution)/shard_map/pallas_call | solution.py:177
  169.3 9.5 %shard_map.46 = (f32[4,32,64,128]{3,2,1,0:T(8,128)}, f32[32,64,128]{2,1,0:T(8,128)}, f32[32,64,128]{2,1,0:T(8,128)}, f32[4,32,1,128]{3,2,1,0:T(1,128)S(1)}, f32[...) custom-call(f32[4,32,64,128]{3,2,1,0:T(8,128)} %get-tuple-element.67.xlo.c.cl.cr, ...), custom_call_target="tpu_custom_call" | custom-call | flops 14680064 | bytes 12582912 | tf_op jit(solution)/shard_map/pallas_call | solution.py:177
  179.5 3.6 %collective-permute-start.36 = (f32[4,32,1,128]{3,2,1,0:T(1,128)S(1)}, f32[4,32,1,128]{3,2,1,0:T(1,128)S(1)}, u32[]{:S(2)}, u32[]{:S(2)}) collective-permute-start(f32[4,32,1,128]{3,2,1,0:T(1,128)S(1)} %get-tuple-element.86), channel_id=1, source_target_pairs={{0,1},{1,2},{2,3},{4,5},{5,6},{6,7},{8,9},{9,10},{10,11},{12,13},{... | collective-permute-start | bytes 196616 | tf_op jit(solution)/shard_map/ppermute | solution.py:192
  185.0 3.6 %collective-permute-done.37.zhi = f32[4,32,1,128]{3,2,1,0:T(1,128)S(1)} collective-permute-done((f32[4,32,1,128]{3,2,1,0:T(1,128)S(1)}, f32[4,32,1,128]{3,2,1,0:T(1,128)S(1)}, u32[]{:S(2)}, u32[]{:S(2)}) %collective-permute-start.37) | collective-permute-done | bytes 65568 | tf_op jit(solution)/shard_map/ppermute | solution.py:192
  188.7 7.3 %shard_map.50 = f32[32,64,128]{2,1,0:T(8,128)S(1)} custom-call(s32[1]{0:T(128)} %bitcast.place, f32[4,32,64,128]{3,2,1,0:T(8,128)} %get-tuple-element.79.c.cl.cr.xlo, f32[4,32,64,128]{3,2,1,0:T(8,128)} %get-tuple-element.79.c.cl.cr.xlo, f32[4,32,64,128]{3,2,1,0:T(8,128)} %get-tuple-element.79.c.cl.cr.xlo, f32[4,64,64,128]{3,2,1,0:T(8,128)} %k.19, ...), custom_call_target="tpu_custom_call" | custom-call | flops 14680064 | bytes 12582912 | tf_op jit(solution)/shard_map/pallas_call | solution.py:177
  198.0 3.6 %collective-permute-start.30 = (f32[4,1,64,128]{3,2,1,0:T(8,128)S(1)}, f32[4,1,64,128]{3,2,1,0:T(8,128)S(1)}, u32[]{:S(2)}, u32[]{:S(2)}) collective-permute-start(f32[4,1,64,128]{3,2,1,0:T(8,128)S(1)} %copy-done.7), channel_id=1, source_target_pairs={{4,0},{8,4},{12,8},{16,12},{20,16},{24,20},{28,24},{5,1},{9,5},{13... | collective-permute-start | bytes 393224 | tf_op jit(solution)/shard_map/ppermute | solution.py:238
  209.7 4.3 %collective-permute-start.34 = (f32[32,64,128]{2,1,0:T(8,128)}, f32[32,64,128]{2,1,0:T(8,128)}, u32[]{:S(2)}, u32[]{:S(2)}) collective-permute-start(f32[32,64,128]{2,1,0:T(8,128)} %get-tuple-element.84), channel_id=1, source_target_pairs={{32,0},{64,32},{96,64},{33,1},{65,33},{97,65},{34,2},{66,34},{98,6... | collective-permute-start | bytes 3145736 | tf_op jit(solution)/shard_map/ppermute | solution.py:189
  214.0 8.1 %shard_map.49 = f32[32,64,128]{2,1,0:T(8,128)} custom-call(s32[1]{0:T(128)} %bitcast.place, f32[4,32,64,128]{3,2,1,0:T(8,128)} %get-tuple-element.71.xhi.c.cl.cr, f32[4,32,64,128]{3,2,1,0:T(8,128)} %get-tuple-element.71.xhi.c.cl.cr, f32[4,32,64,128]{3,2,1,0:T(8,128)} %get-tuple-element.71.xhi.c.cl.cr, f32[4,64,64,128]{3,2,1,0:T(8,128)} %k.19, ...), custom_call_target="tpu_custom_call" | custom-call | flops 14680064 | bytes 12582912 | tf_op jit(solution)/shard_map/pallas_call | solution.py:177
  229.3 16.2 %collective-permute-done.33.ylo = f32[32,64,128]{2,1,0:T(8,128)} collective-permute-done((f32[32,64,128]{2,1,0:T(8,128)}, f32[32,64,128]{2,1,0:T(8,128)}, u32[]{:S(2)}, u32[]{:S(2)}) %collective-permute-start.33) | collective-permute-done | bytes 1048608 | tf_op jit(solution)/shard_map/ppermute | solution.py:189
  252.1 10.5 %shard_map.47 = (f32[4,64,64,128]{3,2,1,0:T(8,128)}, f32[4,32,64,128]{3,2,1,0:T(8,128)}) custom-call(s32[1]{0:T(128)} %bitcast.place, f32[4,32,64,128]{3,2,1,0:T(8,128)} %get-tuple-element.79.c.cl.cr.xlo, f32[4,32,64,128]{3,2,1,0:T(8,128)} %get-tuple-element.79.c.cl.cr.xlo, f32[4,32,64,128]{3,2,1,0:T(8,128)} %get-tuple-element.79.c.cl.cr.xlo, ...), custom_call_target="tpu_custom_call" | custom-call | flops 18874368 | bytes 12582912 | tf_op jit(solution)/shard_map/pallas_call | solution.py:177
  262.6 5.3 %collective-permute-done.23.ylo = f32[32,64,128]{2,1,0:T(8,128)S(1)} collective-permute-done((f32[32,64,128]{2,1,0:T(8,128)}, f32[32,64,128]{2,1,0:T(8,128)S(1)}, u32[]{:S(2)}, u32[]{:S(2)}) %collective-permute-start.23) | collective-permute-done | bytes 1048608 | tf_op jit(solution)/shard_map/ppermute | solution.py:189
  268.0 10.2 %shard_map.48 = (f32[4,64,64,128]{3,2,1,0:T(8,128)}, f32[4,32,64,128]{3,2,1,0:T(8,128)}) custom-call(s32[1]{0:T(128)} %bitcast.place, f32[4,32,64,128]{3,2,1,0:T(8,128)} %get-tuple-element.71.xhi.c.cl.cr, f32[4,32,64,128]{3,2,1,0:T(8,128)} %get-tuple-element.71.xhi.c.cl.cr, ...), custom_call_target="tpu_custom_call", output_to_operand_aliasing={{0}: (11, {})} | custom-call | flops 18874368 | bytes 12582912 | tf_op jit(solution)/shard_map/pallas_call | solution.py:177
  278.2 3.7 %collective-permute-done.43.three = f32[32,64,128]{2,1,0:T(8,128)S(1)} collective-permute-done((f32[32,64,128]{2,1,0:T(8,128)S(1)}, f32[32,64,128]{2,1,0:T(8,128)S(1)}, u32[]{:S(2)}, u32[]{:S(2)}) %collective-permute-start.43) | collective-permute-done | bytes 1048608 | tf_op jit(solution)/shard_map/ppermute | solution.py:247
  281.9 6.7 %shard_map.51.rest_0_ = f32[4,64,64,128]{3,2,1,0:T(8,128)} custom-call(s32[1]{0:T(128)} %bitcast.place, f32[4,32,64,128]{3,2,1,0:T(8,128)} %get-tuple-element.90.sums, f32[32,64,128]{2,1,0:T(8,128)S(1)} %collective-permute-done.41.one, f32[32,64,128]{2,1,0:T(8,128)S(1)} %collective-permute-done.42.two, f32[32,64,128]{2,1,0:T(8,128)S(1)} %collective-permute-done.43.three), custom_call_target="tpu_custom_call" | custom-call | flops 3145728 | bytes 12582912 | tf_op jit(solution)/shard_map/pallas_call | solution.py:177
  288.6 9.8 %collective-permute-done.38.one = f32[32,64,128]{2,1,0:T(8,128)S(1)} collective-permute-done((f32[32,64,128]{2,1,0:T(8,128)}, f32[32,64,128]{2,1,0:T(8,128)S(1)}, u32[]{:S(2)}, u32[]{:S(2)}) %collective-permute-start.38) | collective-permute-done | bytes 1048608 | tf_op jit(solution)/shard_map/ppermute | solution.py:248
  298.4 4.0 %collective-permute-done.40.three = f32[32,64,128]{2,1,0:T(8,128)S(1)} collective-permute-done((f32[32,64,128]{2,1,0:T(8,128)}, f32[32,64,128]{2,1,0:T(8,128)S(1)}, u32[]{:S(2)}, u32[]{:S(2)}) %collective-permute-start.40) | collective-permute-done | bytes 1048608 | tf_op jit(solution)/shard_map/ppermute | solution.py:249
  302.4 6.8 %shard_map.52 = f32[4,64,64,128]{3,2,1,0:T(8,128)} custom-call(s32[1]{0:T(128)} %bitcast.place, f32[4,32,64,128]{3,2,1,0:T(8,128)} %get-tuple-element.89.sums, f32[32,64,128]{2,1,0:T(8,128)S(1)} %collective-permute-done.38.one, f32[32,64,128]{2,1,0:T(8,128)} %collective-permute-done.39.two, ...), custom_call_target="tpu_custom_call", output_to_operand_aliasing={{}: (5, {})} | custom-call | flops 3145728 | bytes 12582912 | tf_op jit(solution)/shard_map/pallas_call | solution.py:177
  (99 shorter events, 95.2 us)
Async XLA Ops:
  4.2 38.6 %collective-permute-start = (f32[32,64,128]{2,1,0:T(8,128)S(1)}, f32[32,64,128]{2,1,0:T(8,128)S(1)}, u32[]{:S(2)}, u32[]{:S(2)}) collective-permute-start(f32[32,64,128]{2,1,0:T(8,128)S(1)} %get-tuple-element.48), channel_id=1, source_target_pairs={{0,32},{32,64},{64,96},{1,33},{33,65},{65,97},{2,34},{34,66},{66,9... | collective-permute-start | bytes 3145736 | tf_op jit(solution)/shard_map/ppermute | solution.py:189
  7.5 35.3 %collective-permute-start.1 = (f32[32,64,128]{2,1,0:T(8,128)S(1)}, f32[32,64,128]{2,1,0:T(8,128)S(1)}, u32[]{:S(2)}, u32[]{:S(2)}) collective-permute-start(f32[32,64,128]{2,1,0:T(8,128)S(1)} %get-tuple-element.49), channel_id=1, source_target_pairs={{32,0},{64,32},{96,64},{33,1},{65,33},{97,65},{34,2},{66,34},{98,6... | collective-permute-start | bytes 3145736 | tf_op jit(solution)/shard_map/ppermute | solution.py:189
  9.5 47.5 %collective-permute-start.7 = (f32[32,64,128]{2,1,0:T(8,128)S(1)}, f32[32,64,128]{2,1,0:T(8,128)S(1)}, u32[]{:S(2)}, u32[]{:S(2)}) collective-permute-start(f32[32,64,128]{2,1,0:T(8,128)S(1)} %get-tuple-element.53), channel_id=1, source_target_pairs={{0,32},{32,64},{64,96},{1,33},{33,65},{65,97},{2,34},{34,66},{66,9... | collective-permute-start | bytes 3145736 | tf_op jit(solution)/shard_map/ppermute | solution.py:189
  12.8 44.2 %collective-permute-start.8 = (f32[32,64,128]{2,1,0:T(8,128)S(1)}, f32[32,64,128]{2,1,0:T(8,128)S(1)}, u32[]{:S(2)}, u32[]{:S(2)}) collective-permute-start(f32[32,64,128]{2,1,0:T(8,128)S(1)} %get-tuple-element.54), channel_id=1, source_target_pairs={{32,0},{64,32},{96,64},{33,1},{65,33},{97,65},{34,2},{66,34},{98,6... | collective-permute-start | bytes 3145736 | tf_op jit(solution)/shard_map/ppermute | solution.py:189
  23.4 7.3 %collective-permute-start.4 = (f32[4,64,1,128]{3,2,1,0:T(1,128)S(1)}, f32[4,64,1,128]{3,2,1,0:T(1,128)S(1)}, u32[]{:S(2)}, u32[]{:S(2)}) collective-permute-start(f32[4,64,1,128]{3,2,1,0:T(1,128)S(1)} %get-tuple-element.94), channel_id=1, source_target_pairs={{1,0},{2,1},{3,2},{5,4},{6,5},{7,6},{9,8},{10,9},{11,10},{13,12},{... | collective-permute-start | bytes 393224 | tf_op jit(solution)/shard_map/ppermute | solution.py:192
  36.6 20.3 %collective-permute-start.9 = (f32[4,1,64,128]{3,2,1,0:T(8,128)S(1)}, f32[4,1,64,128]{3,2,1,0:T(8,128)S(1)}, u32[]{:S(2)}, u32[]{:S(2)}) collective-permute-start(f32[4,1,64,128]{3,2,1,0:T(8,128)S(1)} %get-tuple-element.92), channel_id=1, source_target_pairs={{0,4},{4,8},{8,12},{12,16},{16,20},{20,24},{24,28},{1,5},{5,9},{9,... | collective-permute-start | bytes 393224 | tf_op jit(solution)/shard_map/ppermute | solution.py:204
  51.7 40.5 %collective-permute-start.5 = (f32[32,64,128]{2,1,0:T(8,128)S(1)}, f32[32,64,128]{2,1,0:T(8,128)S(1)}, u32[]{:S(2)}, u32[]{:S(2)}) collective-permute-start(f32[32,64,128]{2,1,0:T(8,128)S(1)} %get-tuple-element.51), channel_id=1, source_target_pairs={{0,32},{32,64},{64,96},{1,33},{33,65},{65,97},{2,34},{34,66},{66,9... | collective-permute-start | bytes 3145736 | tf_op jit(solution)/shard_map/ppermute | solution.py:189
  55.0 44.2 %collective-permute-start.6 = (f32[32,64,128]{2,1,0:T(8,128)S(1)}, f32[32,64,128]{2,1,0:T(8,128)S(1)}, u32[]{:S(2)}, u32[]{:S(2)}) collective-permute-start(f32[32,64,128]{2,1,0:T(8,128)S(1)} %get-tuple-element.52), channel_id=1, source_target_pairs={{32,0},{64,32},{96,64},{33,1},{65,33},{97,65},{34,2},{66,34},{98,6... | collective-permute-start | bytes 3145736 | tf_op jit(solution)/shard_map/ppermute | solution.py:189
  65.9 49.5 %collective-permute-start.15 = (f32[32,64,128]{2,1,0:T(8,128)S(1)}, f32[32,64,128]{2,1,0:T(8,128)S(1)}, u32[]{:S(2)}, u32[]{:S(2)}) collective-permute-start(f32[32,64,128]{2,1,0:T(8,128)S(1)} %get-tuple-element.62), channel_id=1, source_target_pairs={{0,32},{32,64},{64,96},{1,33},{33,65},{65,97},{2,34},{34,66},{66,9... | collective-permute-start | bytes 3145736 | tf_op jit(solution)/shard_map/ppermute | solution.py:189
  69.3 46.1 %collective-permute-start.16 = (f32[32,64,128]{2,1,0:T(8,128)S(1)}, f32[32,64,128]{2,1,0:T(8,128)S(1)}, u32[]{:S(2)}, u32[]{:S(2)}) collective-permute-start(f32[32,64,128]{2,1,0:T(8,128)S(1)} %get-tuple-element.63), channel_id=1, source_target_pairs={{32,0},{64,32},{96,64},{33,1},{65,33},{97,65},{34,2},{66,34},{98,6... | collective-permute-start | bytes 3145736 | tf_op jit(solution)/shard_map/ppermute | solution.py:189
  89.9 20.3 %collective-permute-start.18 = (f32[4,32,1,128]{3,2,1,0:T(1,128)S(1)}, f32[4,32,1,128]{3,2,1,0:T(1,128)S(1)}, u32[]{:S(2)}, u32[]{:S(2)}) collective-permute-start(f32[4,32,1,128]{3,2,1,0:T(1,128)S(1)} %get-tuple-element.65), channel_id=1, source_target_pairs={{0,1},{1,2},{2,3},{4,5},{5,6},{6,7},{8,9},{9,10},{10,11},{12,13},{... | collective-permute-start | bytes 196616 | tf_op jit(solution)/shard_map/ppermute | solution.py:192
  92.2 23.2 %collective-permute-start.17 = (f32[4,1,64,128]{3,2,1,0:T(8,128)S(1)}, f32[4,1,64,128]{3,2,1,0:T(8,128)S(1)}, u32[]{:S(2)}, u32[]{:S(2)}) collective-permute-start(f32[4,1,64,128]{3,2,1,0:T(8,128)S(1)} %get-tuple-element.64), channel_id=1, source_target_pairs={{0,4},{4,8},{8,12},{12,16},{16,20},{20,24},{24,28},{1,5},{5,9},{9,... | collective-permute-start | bytes 393224 | tf_op jit(solution)/shard_map/ppermute | solution.py:238
  99.3 12.7 %collective-permute-start.19 = (f32[4,32,1,128]{3,2,1,0:T(1,128)S(1)}, f32[4,32,1,128]{3,2,1,0:T(1,128)S(1)}, u32[]{:S(2)}, u32[]{:S(2)}) collective-permute-start(f32[4,32,1,128]{3,2,1,0:T(1,128)S(1)} %get-tuple-element.66), channel_id=1, source_target_pairs={{1,0},{2,1},{3,2},{5,4},{6,5},{7,6},{9,8},{10,9},{11,10},{13,12},{... | collective-permute-start | bytes 196616 | tf_op jit(solution)/shard_map/ppermute | solution.py:192
  110.1 43.4 %collective-permute-start.13 = (f32[32,64,128]{2,1,0:T(8,128)S(1)}, f32[32,64,128]{2,1,0:T(8,128)S(1)}, u32[]{:S(2)}, u32[]{:S(2)}) collective-permute-start(f32[32,64,128]{2,1,0:T(8,128)S(1)} %get-tuple-element.60), channel_id=1, source_target_pairs={{0,32},{32,64},{64,96},{1,33},{33,65},{65,97},{2,34},{34,66},{66,9... | collective-permute-start | bytes 3145736 | tf_op jit(solution)/shard_map/ppermute | solution.py:189
  112.0 44.4 %collective-permute-start.14 = (f32[32,64,128]{2,1,0:T(8,128)S(1)}, f32[32,64,128]{2,1,0:T(8,128)S(1)}, u32[]{:S(2)}, u32[]{:S(2)}) collective-permute-start(f32[32,64,128]{2,1,0:T(8,128)S(1)} %get-tuple-element.61), channel_id=1, source_target_pairs={{32,0},{64,32},{96,64},{33,1},{65,33},{97,65},{34,2},{66,34},{98,6... | collective-permute-start | bytes 3145736 | tf_op jit(solution)/shard_map/ppermute | solution.py:189
  124.4 44.9 %collective-permute-start.25 = (f32[32,64,128]{2,1,0:T(8,128)S(1)}, f32[32,64,128]{2,1,0:T(8,128)S(1)}, u32[]{:S(2)}, u32[]{:S(2)}) collective-permute-start(f32[32,64,128]{2,1,0:T(8,128)S(1)} %get-tuple-element.74), channel_id=1, source_target_pairs={{0,32},{32,64},{64,96},{1,33},{33,65},{65,97},{2,34},{34,66},{66,9... | collective-permute-start | bytes 3145736 | tf_op jit(solution)/shard_map/ppermute | solution.py:189
  126.3 42.9 %collective-permute-start.26 = (f32[32,64,128]{2,1,0:T(8,128)S(1)}, f32[32,64,128]{2,1,0:T(8,128)S(1)}, u32[]{:S(2)}, u32[]{:S(2)}) collective-permute-start(f32[32,64,128]{2,1,0:T(8,128)S(1)} %get-tuple-element.75), channel_id=1, source_target_pairs={{32,0},{64,32},{96,64},{33,1},{65,33},{97,65},{34,2},{66,34},{98,6... | collective-permute-start | bytes 3145736 | tf_op jit(solution)/shard_map/ppermute | solution.py:189
  148.2 21.0 %collective-permute-start.27 = (f32[4,1,64,128]{3,2,1,0:T(8,128)S(1)}, f32[4,1,64,128]{3,2,1,0:T(8,128)S(1)}, u32[]{:S(2)}, u32[]{:S(2)}) collective-permute-start(f32[4,1,64,128]{3,2,1,0:T(8,128)S(1)} %get-tuple-element.76), channel_id=1, source_target_pairs={{0,4},{4,8},{8,12},{12,16},{16,20},{20,24},{24,28},{1,5},{5,9},{9,... | collective-permute-start | bytes 393224 | tf_op jit(solution)/shard_map/ppermute | solution.py:238
  153.6 13.8 %collective-permute-start.28 = (f32[4,32,1,128]{3,2,1,0:T(1,128)S(1)}, f32[4,32,1,128]{3,2,1,0:T(1,128)S(1)}, u32[]{:S(2)}, u32[]{:S(2)}) collective-permute-start(f32[4,32,1,128]{3,2,1,0:T(1,128)S(1)} %get-tuple-element.77), channel_id=1, source_target_pairs={{0,1},{1,2},{2,3},{4,5},{5,6},{6,7},{8,9},{9,10},{10,11},{12,13},{... | collective-permute-start | bytes 196616 | tf_op jit(solution)/shard_map/ppermute | solution.py:192
  156.5 12.8 %collective-permute-start.29 = (f32[4,32,1,128]{3,2,1,0:T(1,128)S(1)}, f32[4,32,1,128]{3,2,1,0:T(1,128)S(1)}, u32[]{:S(2)}, u32[]{:S(2)}) collective-permute-start(f32[4,32,1,128]{3,2,1,0:T(1,128)S(1)} %get-tuple-element.78), channel_id=1, source_target_pairs={{1,0},{2,1},{3,2},{5,4},{6,5},{7,6},{9,8},{10,9},{11,10},{13,12},{... | collective-permute-start | bytes 196616 | tf_op jit(solution)/shard_map/ppermute | solution.py:192
  167.3 21.4 %collective-permute-start.35 = (f32[4,1,64,128]{3,2,1,0:T(8,128)S(1)}, f32[4,1,64,128]{3,2,1,0:T(8,128)S(1)}, u32[]{:S(2)}, u32[]{:S(2)}) collective-permute-start(f32[4,1,64,128]{3,2,1,0:T(8,128)S(1)} %get-tuple-element.85), channel_id=1, source_target_pairs={{0,4},{4,8},{8,12},{12,16},{16,20},{20,24},{24,28},{1,5},{5,9},{9,... | collective-permute-start | bytes 393224 | tf_op jit(solution)/shard_map/ppermute | solution.py:238
  196.0 27.8 %collective-permute-start.41 = (f32[32,64,128]{2,1,0:T(8,128)S(1)}, f32[32,64,128]{2,1,0:T(8,128)S(1)}, u32[]{:S(2)}, u32[]{:S(2)}) collective-permute-start(f32[32,64,128]{2,1,0:T(8,128)S(1)} %shard_map.50), channel_id=1, source_target_pairs={{0,32},{32,64},{1,33},{33,65},{2,34},{34,66},{3,35},{35,67},{4,36}... | collective-permute-start | bytes 3145736 | tf_op jit(solution)/shard_map/ppermute | solution.py:244
  197.3 28.4 %collective-permute-start.42 = (f32[32,64,128]{2,1,0:T(8,128)S(1)}, f32[32,64,128]{2,1,0:T(8,128)S(1)}, u32[]{:S(2)}, u32[]{:S(2)}) collective-permute-start(f32[32,64,128]{2,1,0:T(8,128)S(1)} %shard_map.50), channel_id=1, source_target_pairs={{0,96},{1,97},{2,98},{3,99},{4,100},{5,101},{6,102},{7,103},{8,104... | collective-permute-start | bytes 3145736 | tf_op jit(solution)/shard_map/ppermute | solution.py:245
  198.0 16.0 %collective-permute-start.30 = (f32[4,1,64,128]{3,2,1,0:T(8,128)S(1)}, f32[4,1,64,128]{3,2,1,0:T(8,128)S(1)}, u32[]{:S(2)}, u32[]{:S(2)}) collective-permute-start(f32[4,1,64,128]{3,2,1,0:T(8,128)S(1)} %copy-done.7), channel_id=1, source_target_pairs={{4,0},{8,4},{12,8},{16,12},{20,16},{24,20},{28,24},{5,1},{9,5},{13... | collective-permute-start | bytes 393224 | tf_op jit(solution)/shard_map/ppermute | solution.py:238
  206.0 39.5 %collective-permute-start.33 = (f32[32,64,128]{2,1,0:T(8,128)}, f32[32,64,128]{2,1,0:T(8,128)}, u32[]{:S(2)}, u32[]{:S(2)}) collective-permute-start(f32[32,64,128]{2,1,0:T(8,128)} %get-tuple-element.83), channel_id=1, source_target_pairs={{0,32},{32,64},{64,96},{1,33},{33,65},{65,97},{2,34},{34,66},{66,9... | collective-permute-start | bytes 3145736 | tf_op jit(solution)/shard_map/ppermute | solution.py:189
  209.7 37.7 %collective-permute-start.34 = (f32[32,64,128]{2,1,0:T(8,128)}, f32[32,64,128]{2,1,0:T(8,128)}, u32[]{:S(2)}, u32[]{:S(2)}) collective-permute-start(f32[32,64,128]{2,1,0:T(8,128)} %get-tuple-element.84), channel_id=1, source_target_pairs={{32,0},{64,32},{96,64},{33,1},{65,33},{97,65},{34,2},{66,34},{98,6... | collective-permute-start | bytes 3145736 | tf_op jit(solution)/shard_map/ppermute | solution.py:189
  222.1 28.7 %collective-permute-start.39 = (f32[32,64,128]{2,1,0:T(8,128)}, f32[32,64,128]{2,1,0:T(8,128)}, u32[]{:S(2)}, u32[]{:S(2)}) collective-permute-start(f32[32,64,128]{2,1,0:T(8,128)} %shard_map.49), channel_id=1, source_target_pairs={{0,96},{32,0},{1,97},{33,1},{2,98},{34,2},{3,99},{35,3},{4,100},{3... | collective-permute-start | bytes 3145736 | tf_op jit(solution)/shard_map/ppermute | solution.py:243
  223.7 44.2 %collective-permute-start.23 = (f32[32,64,128]{2,1,0:T(8,128)}, f32[32,64,128]{2,1,0:T(8,128)S(1)}, u32[]{:S(2)}, u32[]{:S(2)}) collective-permute-start(f32[32,64,128]{2,1,0:T(8,128)} %copy-done.5), channel_id=1, source_target_pairs={{0,32},{32,64},{64,96},{1,33},{33,65},{65,97},{2,34},{34,66},{66,9... | collective-permute-start | bytes 3145736 | tf_op jit(solution)/shard_map/ppermute | solution.py:189
  225.7 42.3 %collective-permute-start.24 = (f32[32,64,128]{2,1,0:T(8,128)}, f32[32,64,128]{2,1,0:T(8,128)S(1)}, u32[]{:S(2)}, u32[]{:S(2)}) collective-permute-start(f32[32,64,128]{2,1,0:T(8,128)} %copy-done.4), channel_id=1, source_target_pairs={{32,0},{64,32},{96,64},{33,1},{65,33},{97,65},{34,2},{66,34},{98,6... | collective-permute-start | bytes 3145736 | tf_op jit(solution)/shard_map/ppermute | solution.py:189
  245.5 36.4 %collective-permute-start.43 = (f32[32,64,128]{2,1,0:T(8,128)S(1)}, f32[32,64,128]{2,1,0:T(8,128)S(1)}, u32[]{:S(2)}, u32[]{:S(2)}) collective-permute-start(f32[32,64,128]{2,1,0:T(8,128)S(1)} %add_select_fusion), channel_id=1, source_target_pairs={{64,96},{96,64},{65,97},{97,65},{66,98},{98,66},{67,99},{99,67},{6... | collective-permute-start | bytes 3145736 | tf_op jit(solution)/shard_map/ppermute | solution.py:247
  247.4 51.0 %collective-permute-start.38 = (f32[32,64,128]{2,1,0:T(8,128)}, f32[32,64,128]{2,1,0:T(8,128)S(1)}, u32[]{:S(2)}, u32[]{:S(2)}) collective-permute-start(f32[32,64,128]{2,1,0:T(8,128)} %shard_map.49), channel_id=1, source_target_pairs={{0,32},{32,64},{64,96},{1,33},{33,65},{65,97},{2,34},{34,66},{66,9... | collective-permute-start | bytes 3145736 | tf_op jit(solution)/shard_map/ppermute | solution.py:248
  250.8 51.6 %collective-permute-start.40 = (f32[32,64,128]{2,1,0:T(8,128)}, f32[32,64,128]{2,1,0:T(8,128)S(1)}, u32[]{:S(2)}, u32[]{:S(2)}) collective-permute-start(f32[32,64,128]{2,1,0:T(8,128)} %collective-permute-done.39.two), channel_id=1, source_target_pairs={{96,64},{0,96},{97,65},{1,97},{98,66},{2,98},{99,67},{3,99},{100,6... | collective-permute-start | bytes 3145736 | tf_op jit(solution)/shard_map/ppermute | solution.py:249
  (24 other events, 261.2 us)

commit v3 on v0

v3 whole, which is shorter than its diff:
```python
import functools
from typing import NamedTuple

import jax
import jax.numpy as jnp
from jax import lax
from jax.experimental import pallas as pl
from jax.experimental.pallas import tpu as pltpu
from jax.sharding import PartitionSpec as P


STEPS = 4
CHUNKS = 2
PLANES = 4
LIMIT = 8 * 2**20

VMEM = pl.BlockSpec(memory_space=pltpu.VMEM)
SMEM = pl.BlockSpec(memory_space=pltpu.SMEM)
ANY = pl.BlockSpec(memory_space=pl.ANY)


class At(NamedTuple):
    c: int
    k: int
    xlo: int
    xhi: int


def blocks(size, make, done=None):
    def block(i, carry):
        for xx in range(PLANES):
            make(i * PLANES + xx, xx == 0, xx == PLANES - 1)
        if done is not None:
            done(i)
        return carry

    lax.fori_loop(0, size // PLANES, block, 0)


def stencil(c, k, ylo, yhi, xlo, xhi, zlo, zhi, at, size, masked_low):
    rows, _, zs, lanes = c.shape
    z = lax.broadcasted_iota(jnp.int32, (zs, lanes), 0)

    def plane(y, x, first, last):
        mid = c[y, at.c + x]
        if first:
            left = jnp.where(x == 0, xlo[y, at.xlo], c[y, at.c + jnp.maximum(x - 1, 0)])
        else:
            left = c[y, at.c + x - 1]
        if last:
            right = jnp.where(x == size - 1, xhi[y, at.xhi], c[y, at.c + jnp.minimum(x + 1, size - 1)])
        else:
            right = c[y, at.c + x + 1]
        down = jnp.where(z == 0, zlo[y, at.k + x], pltpu.roll(mid, 1, 0))
        up = jnp.where(z == zs - 1, zhi[y, at.k + x], pltpu.roll(mid, zs - 1, 0))
        if y > 0:
            before = c[y - 1, at.c + x]
        elif ylo is None:
            before = masked_low * mid
        else:
            before = ylo[x]
        if y < rows - 1:
            after = c[y + 1, at.c + x]
        elif yhi is None:
            after = mid
        else:
            after = yhi[x]
        around = ((before + after) + (left + right)) + (down + up)
        return mid * (0.6 - (0.2 * mid) * k[y, at.k + x]) + 0.1 * around

    return plane


def step_kernel(place, c, k, ylo, yhi, xlo, xhi, zlo, zhi, *rest, at, edge_x):
    out, row_lo, row_hi, zlo_out, zhi_out, edge = rest[-6:]
    size = out.shape[1]
    rows, _, zs, _ = c.shape
    plane = stencil(c, k, ylo, yhi, xlo, xhi, zlo, zhi, at, size, None)

    def make(x, first, last):
        for y in range(rows):
            new = plane(y, x, first, last)
            out[y, x] = new
            zlo_out[y, at.k + x] = new[0:1]
            zhi_out[y, at.k + x] = new[zs - 1 : zs]
            if y == 0:
                row_lo[x] = new
            if y == rows - 1:
                row_hi[x] = new

    blocks(size, make)
    for y in range(rows):
        edge[y, 0] = out[y, edge_x]


def total_kernel(place, c, k, xlo, xhi, zlo, zhi, total, *, at):
    size = total.shape[0]
    inside = jnp.where(place[0] > 0, 1.0, 0.0).astype(jnp.float32)
    plane = stencil(c, k, None, None, xlo, xhi, zlo, zhi, at, size, inside)

    def make(x, first, last):
        value = plane(0, x, first, last)
        for y in range(1, c.shape[0]):
            value = value + plane(y, x, first, last)
        total[x] = value

    blocks(size, make)


def copies(held, out, sems, at):
    def copy(i):
        there = pl.ds(at.k + i * PLANES, PLANES)
        return pltpu.make_async_copy(held.at[:, pl.ds(i * PLANES, PLANES)], out.at[:, there], sems.at[i])

    return copy


def finish(copy, size):
    def wait(i, carry):
        copy(i).wait()
        return carry

    lax.fori_loop(0, size // PLANES, wait, 0)


def last_kernel(place, c, k, ylo, yhi, xlo, xhi, zlo, zhi, *rest, at):
    out, sums, held, sems = rest[-4:]
    size = sums.shape[1]
    inside = jnp.where(place[0] > 0, 0.1, 0.0).astype(jnp.float32)
    plane = stencil(c, k, ylo, yhi, xlo, xhi, zlo, zhi, at, size, None)
    copy = copies(held, out, sems, at)

    def make(x, first, last):
        sofar = inside * c[0, at.c + x] - 0.1 * ylo[x]
        for y in range(c.shape[0]):
            new = plane(y, x, first, last)
            held[y, x] = new
            sofar = sofar + new
            sums[y, x] = sofar

    blocks(size, make, lambda i: copy(i).start())
    finish(copy, size)


def add_kernel(place, sums, one, two, three, *rest, at, scale):
    out, held, sems = rest[-3:]
    rows, size, _, _ = sums.shape
    inside = jnp.where(place[0] > 0, 1.0, 0.0).astype(jnp.float32)
    copy = copies(held, out, sems, at)

    def make(x, first, last):
        below = one[x] + inside * two[x] + three[x]
        for y in range(rows):
            held[y, x] = (sums[y, x] + below) * scale

    blocks(size, make, lambda i: copy(i).start())
    finish(copy, size)


def pass_kernel(place, total, one, two, out):
    def make(x, first, last):
        out[x] = jnp.where(place[0] == 2, total[x] + one[x], two[x])

    blocks(out.shape[0], make)


def shifts(axis):
    count = lax.axis_size(axis)
    up = [(i, i + 1) for i in range(count - 1)]
    return up, [(b, a) for a, b in up]


def program(tracer, crowding):
    rows, xs, zs, lanes = tracer.shape
    n = CHUNKS
    size = xs // n
    cells = rows * size * zs * lanes
    f32 = jnp.float32
    place = lax.axis_index("rows").astype(jnp.int32)
    tracer, place = lax.optimization_barrier((tracer, place))
    here = place.reshape(1)
    row_up, row_down = shifts("rows")
    col_up, col_down = shifts("cols")
    slab_up, slab_down = shifts("slabs")
    chunk_shape = pltpu.VMEM((rows, size, zs, lanes), f32)
    row_shape = pltpu.VMEM((size, zs, lanes), f32)
    edge_shape = pltpu.VMEM((rows, xs, 1, lanes), f32)
    side_shape = pltpu.VMEM((rows, 1, zs, lanes), f32)
    full = jax.ShapeDtypeStruct(tracer.shape, f32)
    scratch = [pltpu.VMEM((rows, size, zs, lanes), f32), pltpu.SemaphoreType.DMA((size // PLANES,))]

    def send_rows(lo, hi):
        return (lax.ppermute(hi, "rows", row_up), lax.ppermute(lo, "rows", row_down))

    def send_sides(low, high, zlow, zhigh):
        x = (lax.ppermute(high, "cols", col_up), lax.ppermute(low, "cols", col_down))
        z = (lax.ppermute(zhigh, "slabs", slab_up), lax.ppermute(zlow, "slabs", slab_down))
        return x, z

    def call(kernel, inputs, out_shape, per_cell, aliased=(), scratch=(), hbm_out=False):
        in_specs = [SMEM if array is here else VMEM for array in inputs] + [ANY if hbm_out else VMEM] * len(aliased)
        first = 0 if hbm_out else 3
        return pl.pallas_call(
            kernel,
            in_specs=in_specs,
            out_specs=[ANY if hbm_out and i == 0 else VMEM for i in range(len(out_shape))],
            out_shape=out_shape,
            input_output_aliases={len(inputs) + i: first + i for i in range(len(aliased))},
            scratch_shapes=list(scratch),
            compiler_params=pltpu.CompilerParams(vmem_limit_bytes=LIMIT),
            cost_estimate=pl.CostEstimate(flops=cells * per_cell, bytes_accessed=cells * 12, transcendentals=0),
        )(*inputs, *aliased)

    halo_y = []
    source = tracer
    for j in range(n):
        lo, hi = (source[r, j * size : (j + 1) * size] for r in (0, rows - 1))
        lo, hi, source = lax.optimization_barrier((lo, hi, source))
        halo_y.append(send_rows(lo, hi))
    halo_x, halo_z = send_sides(tracer[:, 0:1], tracer[:, xs - 1 : xs], tracer[:, :, 0:1], tracer[:, :, zs - 1 : zs])
    field = [tracer] * n
    whole = True

    def near(j):
        base = j * size if whole else 0
        low, xlo = (field[j - 1], (base if whole else size) - 1) if j else (halo_x[0], 0)
        high, xhi = (field[j + 1], base + size if whole else 0) if j < n - 1 else (halo_x[1], 0)
        return [field[j], crowding], [low, high, *halo_z], At(base, j * size, xlo, xhi)

    for _ in range(STEPS - 1):
        made, next_y, edges, z_edges = [], [], [], ()
        for j in range(n):
            first, sides, at = near(j)
            out, lo, hi, zlo, zhi, edge = call(
                functools.partial(step_kernel, at=at, edge_x=size - 1 if j == n - 1 else 0),
                [here, *first, *halo_y[j], *sides],
                [chunk_shape, row_shape, row_shape, edge_shape, edge_shape, side_shape],
                14,
                aliased=z_edges,
            )
            z_edges = (zlo, zhi)
            made.append(out)
            next_y.append(send_rows(lo, hi))
            edges.append(edge)
        halo_x, halo_z = send_sides(edges[0], edges[-1], *z_edges)
        field, halo_y, whole = made, next_y, False

    total = []
    for j in range(n):
        first, sides, at = near(j)
        total += call(functools.partial(total_kernel, at=at), [here, *first, *sides], [row_shape], 14)
    one, two, three = [None] * n, [None] * n, [None] * n
    one[0] = lax.ppermute(total[0], "rows", [(0, 1), (1, 2)])
    two[0] = lax.ppermute(total[0], "rows", [(0, 3)])
    two[1] = lax.ppermute(total[1], "rows", [(0, 3), (1, 0)])
    (passed,) = call(pass_kernel, [here, total[0], one[0], two[0]], [row_shape], 1)
    three[0] = lax.ppermute(passed, "rows", [(2, 3), (3, 2)])
    one[1] = lax.ppermute(total[1], "rows", row_up)
    three[1] = lax.ppermute(two[1], "rows", [(3, 2), (0, 3)])

    end, column = (), ()
    sums = []
    for j in range(n):
        first, sides, at = near(j)
        kernel = functools.partial(last_kernel, at=at)
        inputs = [here, *first, *halo_y[j], *sides]
        *end, partial = call(kernel, inputs, [full, chunk_shape], 18, end, scratch, True)
        sums.append(partial)
    for j in range(n):
        kernel = functools.partial(add_kernel, at=near(j)[2], scale=1.0 / (rows * lax.axis_size("rows")))
        column = call(kernel, [here, sums[j], one[j], two[j], three[j]], [full], 3, column, scratch, True)
    return column[0], end[0]


def solution(mesh):
    spec = P("rows", "cols", "slabs", None)
    return jax.shard_map(program, mesh=mesh, in_specs=(spec, spec), out_specs=(spec, spec), check_vma=False)
```

time: 449 us -> 269 us (0.60)
  the two profiles are of different devices: /device:TPU:1 before, /device:TPU:80 now
where the time goes in v3:
time: 269 us; the launch traced here: 268 us
  waiting for transfers between devices  133 us (49%)
  starting transfers between devices  94 us (35%)
  Pallas kernels  29.2 us (11%)
  local copies, waits for them, and re-layouts  9.78 us (4%)
    ppermute x8, waiting for transfers between devices, send_rows(): lax.ppermute(hi, 'rows', row_up)  41.4 us
    pallas_call x13, Pallas kernels, call(): pl.pallas_call(kernel, in_specs=in_specs, out_specs=[ANY if hbm_out and i...  29.2 us
    ppermute x8, starting transfers between devices, send_rows(): lax.ppermute(lo, 'rows', row_down)  26.9 us
    ppermute x4, waiting for transfers between devices, send_sides(): lax.ppermute(high, 'cols', col_up)  22.6 us
    ppermute x8, starting transfers between devices, send_rows(): lax.ppermute(hi, 'rows', row_up)  20.7 us
    ppermute x1, waiting for transfers between devices, program(): one[0] = lax.ppermute(total[0], 'rows', [(0, 1), (1, 2)])  16.3 us
    ppermute x1, waiting for transfers between devices, program(): one[1] = lax.ppermute(total[1], 'rows', row_up)  15 us
    ppermute x4, waiting for transfers between devices, send_sides(): lax.ppermute(zlow, 'slabs', slab_down)  14.9 us
  transfers between devices with their start and end apart: 38, of which 23 were waited for; matrix products, arithmetic and copies ran while one was open for 2% of the time, Pallas kernels for 9%

profile of v3, /device:TPU:80, one launch (start us, length us, event | category | flops | bytes accessed | tf_op | source)
XLA Modules:
  0.0 267.6 jit_solution(12784081625266437200)
XLA Ops:
  2.5 3.8 %collective-permute-start.5 = (f32[32,64,128]{2,1,0:T(8,128)S(1)}, f32[32,64,128]{2,1,0:T(8,128)S(1)}, u32[]{:S(2)}, u32[]{:S(2)}) collective-permute-start(f32[32,64,128]{2,1,0:T(8,128)S(1)} %get-tuple-element.54), channel_id=1, source_target_pairs={{0,32},{32,64},{64,96},{1,33},{33,65},{65,97},{2,34},{34,66},{66,9... | collective-permute-start | bytes 3145736 | tf_op jit(solution)/shard_map/ppermute | solution.py:193
  10.4 3.6 %collective-permute-start = (f32[32,64,128]{2,1,0:T(8,128)S(1)}, f32[32,64,128]{2,1,0:T(8,128)S(1)}, u32[]{:S(2)}, u32[]{:S(2)}) collective-permute-start(f32[32,64,128]{2,1,0:T(8,128)S(1)} %get-tuple-element.52), channel_id=1, source_target_pairs={{0,32},{32,64},{64,96},{1,33},{33,65},{65,97},{2,34},{34,66},{66,9... | collective-permute-start | bytes 3145736 | tf_op jit(solution)/shard_map/ppermute | solution.py:193
  22.6 3.4 %collective-permute-done.4.zhi = f32[4,64,1,128]{3,2,1,0:T(1,128)S(1)} collective-permute-done((f32[4,64,1,128]{3,2,1,0:T(1,128)S(1)}, f32[4,64,1,128]{3,2,1,0:T(1,128)S(1)}, u32[]{:S(2)}, u32[]{:S(2)}) %collective-permute-start.4) | collective-permute-done | bytes 131104 | tf_op jit(solution)/shard_map/ppermute | solution.py:197
  26.0 3.4 %collective-permute-start.7 = (f32[4,1,64,128]{3,2,1,0:T(8,128)S(1)}, f32[4,1,64,128]{3,2,1,0:T(8,128)S(1)}, u32[]{:S(2)}, u32[]{:S(2)}) collective-permute-start(f32[4,1,64,128]{3,2,1,0:T(8,128)S(1)} %get-tuple-element.96), channel_id=1, source_target_pairs={{0,4},{4,8},{8,12},{12,16},{16,20},{20,24},{24,28},{1,5},{5,9},{9,... | collective-permute-start | bytes 393224 | tf_op jit(solution)/shard_map/ppermute | solution.py:196
  29.4 7.1 %collective-permute-done.7.xlo = f32[4,1,64,128]{3,2,1,0:T(8,128)S(1)} collective-permute-done((f32[4,1,64,128]{3,2,1,0:T(8,128)S(1)}, f32[4,1,64,128]{3,2,1,0:T(8,128)S(1)}, u32[]{:S(2)}, u32[]{:S(2)}) %collective-permute-start.7) | collective-permute-done | bytes 131104 | tf_op jit(solution)/shard_map/ppermute | solution.py:196
  38.4 3.4 %copy-done.1 = f32[4,64,64,128]{3,2,1,0:T(8,128)S(1)} copy-done((f32[4,64,64,128]{3,2,1,0:T(8,128)S(1)}, f32[4,64,64,128]{3,2,1,0:T(8,128)}, u32[]{:S(2)}) %copy-start.1) | copy-done | bytes 8388632
  44.0 3.7 %collective-permute-start.13 = (f32[32,64,128]{2,1,0:T(8,128)S(1)}, f32[32,64,128]{2,1,0:T(8,128)S(1)}, u32[]{:S(2)}, u32[]{:S(2)}) collective-permute-start(f32[32,64,128]{2,1,0:T(8,128)S(1)} %get-tuple-element.65), channel_id=1, source_target_pairs={{0,32},{32,64},{64,96},{1,33},{33,65},{65,97},{2,34},{34,66},{66,9... | collective-permute-start | bytes 3145736 | tf_op jit(solution)/shard_map/ppermute | solution.py:193
  59.5 3.9 %collective-permute-start.9 = (f32[32,64,128]{2,1,0:T(8,128)S(1)}, f32[32,64,128]{2,1,0:T(8,128)S(1)}, u32[]{:S(2)}, u32[]{:S(2)}) collective-permute-start(f32[32,64,128]{2,1,0:T(8,128)S(1)} %get-tuple-element.60), channel_id=1, source_target_pairs={{32,0},{64,32},{96,64},{33,1},{65,33},{97,65},{34,2},{66,34},{98,6... | collective-permute-start | bytes 3145736 | tf_op jit(solution)/shard_map/ppermute | solution.py:193
  66.9 5.8 %collective-permute-done.12.zhi = f32[4,64,1,128]{3,2,1,0:T(1,128)S(1)} collective-permute-done((f32[4,64,1,128]{3,2,1,0:T(1,128)S(1)}, f32[4,64,1,128]{3,2,1,0:T(1,128)S(1)}, u32[]{:S(2)}, u32[]{:S(2)}) %collective-permute-start.12) | collective-permute-done | bytes 131104 | tf_op jit(solution)/shard_map/ppermute | solution.py:197
  72.8 3.4 %collective-permute-start.15 = (f32[4,1,64,128]{3,2,1,0:T(8,128)S(1)}, f32[4,1,64,128]{3,2,1,0:T(8,128)S(1)}, u32[]{:S(2)}, u32[]{:S(2)}) collective-permute-start(f32[4,1,64,128]{3,2,1,0:T(8,128)S(1)} %get-tuple-element.67), channel_id=1, source_target_pairs={{0,4},{4,8},{8,12},{12,16},{16,20},{20,24},{24,28},{1,5},{5,9},{9,... | collective-permute-start | bytes 393224 | tf_op jit(solution)/shard_map/ppermute | solution.py:196
  76.2 7.1 %collective-permute-done.15.xlo = f32[4,1,64,128]{3,2,1,0:T(8,128)S(1)} collective-permute-done((f32[4,1,64,128]{3,2,1,0:T(8,128)S(1)}, f32[4,1,64,128]{3,2,1,0:T(8,128)S(1)}, u32[]{:S(2)}, u32[]{:S(2)}) %collective-permute-start.15) | collective-permute-done | bytes 131104 | tf_op jit(solution)/shard_map/ppermute | solution.py:196
  89.4 3.9 %collective-permute-start.22 = (f32[32,64,128]{2,1,0:T(8,128)S(1)}, f32[32,64,128]{2,1,0:T(8,128)S(1)}, u32[]{:S(2)}, u32[]{:S(2)}) collective-permute-start(f32[32,64,128]{2,1,0:T(8,128)S(1)} %get-tuple-element.78), channel_id=1, source_target_pairs={{32,0},{64,32},{96,64},{33,1},{65,33},{97,65},{34,2},{66,34},{98,6... | collective-permute-start | bytes 3145736 | tf_op jit(solution)/shard_map/ppermute | solution.py:193
  93.3 3.9 %collective-permute-done.8.ylo = f32[32,64,128]{2,1,0:T(8,128)S(1)} collective-permute-done((f32[32,64,128]{2,1,0:T(8,128)S(1)}, f32[32,64,128]{2,1,0:T(8,128)S(1)}, u32[]{:S(2)}, u32[]{:S(2)}) %collective-permute-start.8) | collective-permute-done | bytes 1048608 | tf_op jit(solution)/shard_map/ppermute | solution.py:193
  104.4 3.9 %collective-permute-start.17 = (f32[32,64,128]{2,1,0:T(8,128)S(1)}, f32[32,64,128]{2,1,0:T(8,128)S(1)}, u32[]{:S(2)}, u32[]{:S(2)}) collective-permute-start(f32[32,64,128]{2,1,0:T(8,128)S(1)} %get-tuple-element.72), channel_id=1, source_target_pairs={{32,0},{64,32},{96,64},{33,1},{65,33},{97,65},{34,2},{66,34},{98,6... | collective-permute-start | bytes 3145736 | tf_op jit(solution)/shard_map/ppermute | solution.py:193
  112.0 5.7 %collective-permute-done.20.zhi = f32[4,64,1,128]{3,2,1,0:T(1,128)S(1)} collective-permute-done((f32[4,64,1,128]{3,2,1,0:T(1,128)S(1)}, f32[4,64,1,128]{3,2,1,0:T(1,128)S(1)}, u32[]{:S(2)}, u32[]{:S(2)}) %collective-permute-start.20) | collective-permute-done | bytes 131104 | tf_op jit(solution)/shard_map/ppermute | solution.py:197
  117.7 3.4 %collective-permute-start.23 = (f32[4,1,64,128]{3,2,1,0:T(8,128)S(1)}, f32[4,1,64,128]{3,2,1,0:T(8,128)S(1)}, u32[]{:S(2)}, u32[]{:S(2)}) collective-permute-start(f32[4,1,64,128]{3,2,1,0:T(8,128)S(1)} %get-tuple-element.79), channel_id=1, source_target_pairs={{0,4},{4,8},{8,12},{12,16},{16,20},{20,24},{24,28},{1,5},{5,9},{9,... | collective-permute-start | bytes 393224 | tf_op jit(solution)/shard_map/ppermute | solution.py:196
  121.1 7.1 %collective-permute-done.23.xlo = f32[4,1,64,128]{3,2,1,0:T(8,128)S(1)} collective-permute-done((f32[4,1,64,128]{3,2,1,0:T(8,128)S(1)}, f32[4,1,64,128]{3,2,1,0:T(8,128)S(1)}, u32[]{:S(2)}, u32[]{:S(2)}) %collective-permute-start.23) | collective-permute-done | bytes 131104 | tf_op jit(solution)/shard_map/ppermute | solution.py:196
  135.0 6.9 %collective-permute-done.16.ylo = f32[32,64,128]{2,1,0:T(8,128)S(1)} collective-permute-done((f32[32,64,128]{2,1,0:T(8,128)S(1)}, f32[32,64,128]{2,1,0:T(8,128)S(1)}, u32[]{:S(2)}, u32[]{:S(2)}) %collective-permute-start.16) | collective-permute-done | bytes 1048608 | tf_op jit(solution)/shard_map/ppermute | solution.py:193
  141.9 3.3 %collective-permute-done.17.yhi = f32[32,64,128]{2,1,0:T(8,128)S(1)} collective-permute-done((f32[32,64,128]{2,1,0:T(8,128)S(1)}, f32[32,64,128]{2,1,0:T(8,128)S(1)}, u32[]{:S(2)}, u32[]{:S(2)}) %collective-permute-start.17) | collective-permute-done | bytes 1048608 | tf_op jit(solution)/shard_map/ppermute | solution.py:193
  150.7 3.2 %collective-permute-start.31 = (f32[4,1,64,128]{3,2,1,0:T(8,128)S(1)}, f32[4,1,64,128]{3,2,1,0:T(8,128)S(1)}, u32[]{:S(2)}, u32[]{:S(2)}) collective-permute-start(f32[4,1,64,128]{3,2,1,0:T(8,128)S(1)} %get-tuple-element.91), channel_id=1, source_target_pairs={{0,4},{4,8},{8,12},{12,16},{16,20},{20,24},{24,28},{1,5},{5,9},{9,... | collective-permute-start | bytes 393224 | tf_op jit(solution)/shard_map/ppermute | solution.py:196
  153.9 6.3 %collective-permute-start.26 = (f32[4,1,64,128]{3,2,1,0:T(8,128)S(1)}, f32[4,1,64,128]{3,2,1,0:T(8,128)S(1)}, u32[]{:S(2)}, u32[]{:S(2)}) collective-permute-start(f32[4,1,64,128]{3,2,1,0:T(8,128)S(1)} %get-tuple-element.86), channel_id=1, source_target_pairs={{4,0},{8,4},{12,8},{16,12},{20,16},{24,20},{28,24},{5,1},{9,5},{13... | collective-permute-start | bytes 393224 | tf_op jit(solution)/shard_map/ppermute | solution.py:196
  168.0 4.6 %collective-permute-start.30 = (f32[32,64,128]{2,1,0:T(8,128)S(1)}, f32[32,64,128]{2,1,0:T(8,128)S(1)}, u32[]{:S(2)}, u32[]{:S(2)}) collective-permute-start(f32[32,64,128]{2,1,0:T(8,128)S(1)} %get-tuple-element.90), channel_id=1, source_target_pairs={{32,0},{64,32},{96,64},{33,1},{65,33},{97,65},{34,2},{66,34},{98,6... | collective-permute-start | bytes 3145736 | tf_op jit(solution)/shard_map/ppermute | solution.py:193
  175.6 16.3 %collective-permute-done.35.one = f32[32,64,128]{2,1,0:T(8,128)S(1)} collective-permute-done((f32[32,64,128]{2,1,0:T(8,128)S(1)}, f32[32,64,128]{2,1,0:T(8,128)S(1)}, u32[]{:S(2)}, u32[]{:S(2)}) %collective-permute-start.35) | collective-permute-done | bytes 1048608 | tf_op jit(solution)/shard_map/ppermute | solution.py:253
  193.9 3.9 %collective-permute-start.25 = (f32[32,64,128]{2,1,0:T(8,128)S(1)}, f32[32,64,128]{2,1,0:T(8,128)S(1)}, u32[]{:S(2)}, u32[]{:S(2)}) collective-permute-start(f32[32,64,128]{2,1,0:T(8,128)S(1)} %get-tuple-element.84), channel_id=1, source_target_pairs={{32,0},{64,32},{96,64},{33,1},{65,33},{97,65},{34,2},{66,34},{98,6... | collective-permute-start | bytes 3145736 | tf_op jit(solution)/shard_map/ppermute | solution.py:193
  198.0 16.4 %collective-permute-done.29.ylo = f32[32,64,128]{2,1,0:T(8,128)S(1)} collective-permute-done((f32[32,64,128]{2,1,0:T(8,128)S(1)}, f32[32,64,128]{2,1,0:T(8,128)S(1)}, u32[]{:S(2)}, u32[]{:S(2)}) %collective-permute-start.29) | collective-permute-done | bytes 1048608 | tf_op jit(solution)/shard_map/ppermute | solution.py:193
  216.3 3.9 %collective-permute-start.32 = (f32[32,64,128]{2,1,0:T(8,128)S(1)}, f32[32,64,128]{2,1,0:T(8,128)S(1)}, u32[]{:S(2)}, u32[]{:S(2)}) collective-permute-start(f32[32,64,128]{2,1,0:T(8,128)S(1)} %shard_map.49), channel_id=1, source_target_pairs={{0,32},{32,64},{64,96},{1,33},{33,65},{65,97},{2,34},{34,66},{66,9... | collective-permute-start | bytes 3145736 | tf_op jit(solution)/shard_map/ppermute | solution.py:258
  221.6 3.4 %shard_map.47 = (f32[4,64,64,128]{3,2,1,0:T(8,128)}, f32[4,32,64,128]{3,2,1,0:T(8,128)S(1)}) custom-call(s32[1]{0:T(128)} %bitcast.place, f32[4,32,64,128]{3,2,1,0:T(8,128)S(1)} %get-tuple-element.85.c.xlo, f32[4,64,64,128]{3,2,1,0:T(8,128)S(1)} %copy-done, f32[32,64,128]{2,1,0:T(8,128)S(1)} %collective-permute-done.29.ylo, ...), custom_call_target="tpu_custom_call" | custom-call | flops 18874368 | bytes 12582912 | tf_op jit(solution)/shard_map/pallas_call | solution.py:203
  225.0 11.9 %collective-permute-done.24.ylo = f32[32,64,128]{2,1,0:T(8,128)S(1)} collective-permute-done((f32[32,64,128]{2,1,0:T(8,128)S(1)}, f32[32,64,128]{2,1,0:T(8,128)S(1)}, u32[]{:S(2)}, u32[]{:S(2)}) %collective-permute-start.24) | collective-permute-done | bytes 1048608 | tf_op jit(solution)/shard_map/ppermute | solution.py:193
  236.9 3.4 %shard_map.48 = (f32[4,64,64,128]{3,2,1,0:T(8,128)}, f32[4,32,64,128]{3,2,1,0:T(8,128)S(1)}) custom-call(s32[1]{0:T(128)} %bitcast.place, f32[4,32,64,128]{3,2,1,0:T(8,128)S(1)} %get-tuple-element.82.xhi.c, f32[4,64,64,128]{3,2,1,0:T(8,128)S(1)} %copy-done, f32[32,64,128]{2,1,0:T(8,128)S(1)} %collective-permute-done.24.ylo, ...), custom_call_target="tpu_custom_call", output_to_operand_aliasing={{0}: (9, {})} | custom-call | flops 18874368 | bytes 12582912 | tf_op jit(solution)/shard_map/pallas_call | solution.py:203
  240.3 4.0 %collective-permute-done.37.three = f32[32,64,128]{2,1,0:T(8,128)S(1)} collective-permute-done((f32[32,64,128]{2,1,0:T(8,128)S(1)}, f32[32,64,128]{2,1,0:T(8,128)S(1)}, u32[]{:S(2)}, u32[]{:S(2)}) %collective-permute-start.37) | collective-permute-done | bytes 1048608 | tf_op jit(solution)/shard_map/ppermute | solution.py:257
  246.4 15.0 %collective-permute-done.32.one = f32[32,64,128]{2,1,0:T(8,128)S(1)} collective-permute-done((f32[32,64,128]{2,1,0:T(8,128)S(1)}, f32[32,64,128]{2,1,0:T(8,128)S(1)}, u32[]{:S(2)}, u32[]{:S(2)}) %collective-permute-start.32) | collective-permute-done | bytes 1048608 | tf_op jit(solution)/shard_map/ppermute | solution.py:258
  261.4 4.1 %collective-permute-done.34.three = f32[32,64,128]{2,1,0:T(8,128)S(1)} collective-permute-done((f32[32,64,128]{2,1,0:T(8,128)S(1)}, f32[32,64,128]{2,1,0:T(8,128)S(1)}, u32[]{:S(2)}, u32[]{:S(2)}) %collective-permute-start.34) | collective-permute-done | bytes 1048608 | tf_op jit(solution)/shard_map/ppermute | solution.py:259
  (65 shorter events, 83.7 us)
Async XLA Ops:
  2.5 35.9 %collective-permute-start.5 = (f32[32,64,128]{2,1,0:T(8,128)S(1)}, f32[32,64,128]{2,1,0:T(8,128)S(1)}, u32[]{:S(2)}, u32[]{:S(2)}) collective-permute-start(f32[32,64,128]{2,1,0:T(8,128)S(1)} %get-tuple-element.54), channel_id=1, source_target_pairs={{0,32},{32,64},{64,96},{1,33},{33,65},{65,97},{2,34},{34,66},{66,9... | collective-permute-start | bytes 3145736 | tf_op jit(solution)/shard_map/ppermute | solution.py:193
  6.3 32.1 %collective-permute-start.6 = (f32[32,64,128]{2,1,0:T(8,128)S(1)}, f32[32,64,128]{2,1,0:T(8,128)S(1)}, u32[]{:S(2)}, u32[]{:S(2)}) collective-permute-start(f32[32,64,128]{2,1,0:T(8,128)S(1)} %get-tuple-element.55), channel_id=1, source_target_pairs={{32,0},{64,32},{96,64},{33,1},{65,33},{97,65},{34,2},{66,34},{98,6... | collective-permute-start | bytes 3145736 | tf_op jit(solution)/shard_map/ppermute | solution.py:193
  10.4 41.7 %collective-permute-start = (f32[32,64,128]{2,1,0:T(8,128)S(1)}, f32[32,64,128]{2,1,0:T(8,128)S(1)}, u32[]{:S(2)}, u32[]{:S(2)}) collective-permute-start(f32[32,64,128]{2,1,0:T(8,128)S(1)} %get-tuple-element.52), channel_id=1, source_target_pairs={{0,32},{32,64},{64,96},{1,33},{33,65},{65,97},{2,34},{34,66},{66,9... | collective-permute-start | bytes 3145736 | tf_op jit(solution)/shard_map/ppermute | solution.py:193
  14.0 41.3 %collective-permute-start.1 = (f32[32,64,128]{2,1,0:T(8,128)S(1)}, f32[32,64,128]{2,1,0:T(8,128)S(1)}, u32[]{:S(2)}, u32[]{:S(2)}) collective-permute-start(f32[32,64,128]{2,1,0:T(8,128)S(1)} %get-tuple-element.53), channel_id=1, source_target_pairs={{32,0},{64,32},{96,64},{33,1},{65,33},{97,65},{34,2},{66,34},{98,6... | collective-permute-start | bytes 3145736 | tf_op jit(solution)/shard_map/ppermute | solution.py:193
  26.0 10.5 %collective-permute-start.7 = (f32[4,1,64,128]{3,2,1,0:T(8,128)S(1)}, f32[4,1,64,128]{3,2,1,0:T(8,128)S(1)}, u32[]{:S(2)}, u32[]{:S(2)}) collective-permute-start(f32[4,1,64,128]{3,2,1,0:T(8,128)S(1)} %get-tuple-element.96), channel_id=1, source_target_pairs={{0,4},{4,8},{8,12},{12,16},{16,20},{20,24},{24,28},{1,5},{5,9},{9,... | collective-permute-start | bytes 393224 | tf_op jit(solution)/shard_map/ppermute | solution.py:196
  36.5 13.4 %collective-permute-start.2 = (f32[4,1,64,128]{3,2,1,0:T(8,128)S(1)}, f32[4,1,64,128]{3,2,1,0:T(8,128)S(1)}, u32[]{:S(2)}, u32[]{:S(2)}) collective-permute-start(f32[4,1,64,128]{3,2,1,0:T(8,128)S(1)} %get-tuple-element.97), channel_id=1, source_target_pairs={{4,0},{8,4},{12,8},{16,12},{20,16},{24,20},{28,24},{5,1},{9,5},{13... | collective-permute-start | bytes 393224 | tf_op jit(solution)/shard_map/ppermute | solution.py:196
  44.0 41.1 %collective-permute-start.13 = (f32[32,64,128]{2,1,0:T(8,128)S(1)}, f32[32,64,128]{2,1,0:T(8,128)S(1)}, u32[]{:S(2)}, u32[]{:S(2)}) collective-permute-start(f32[32,64,128]{2,1,0:T(8,128)S(1)} %get-tuple-element.65), channel_id=1, source_target_pairs={{0,32},{32,64},{64,96},{1,33},{33,65},{65,97},{2,34},{34,66},{66,9... | collective-permute-start | bytes 3145736 | tf_op jit(solution)/shard_map/ppermute | solution.py:193
  47.7 37.5 %collective-permute-start.14 = (f32[32,64,128]{2,1,0:T(8,128)S(1)}, f32[32,64,128]{2,1,0:T(8,128)S(1)}, u32[]{:S(2)}, u32[]{:S(2)}) collective-permute-start(f32[32,64,128]{2,1,0:T(8,128)S(1)} %get-tuple-element.66), channel_id=1, source_target_pairs={{32,0},{64,32},{96,64},{33,1},{65,33},{97,65},{34,2},{66,34},{98,6... | collective-permute-start | bytes 3145736 | tf_op jit(solution)/shard_map/ppermute | solution.py:193
  57.5 39.6 %collective-permute-start.8 = (f32[32,64,128]{2,1,0:T(8,128)S(1)}, f32[32,64,128]{2,1,0:T(8,128)S(1)}, u32[]{:S(2)}, u32[]{:S(2)}) collective-permute-start(f32[32,64,128]{2,1,0:T(8,128)S(1)} %get-tuple-element.59), channel_id=1, source_target_pairs={{0,32},{32,64},{64,96},{1,33},{33,65},{65,97},{2,34},{34,66},{66,9... | collective-permute-start | bytes 3145736 | tf_op jit(solution)/shard_map/ppermute | solution.py:193
  59.5 40.8 %collective-permute-start.9 = (f32[32,64,128]{2,1,0:T(8,128)S(1)}, f32[32,64,128]{2,1,0:T(8,128)S(1)}, u32[]{:S(2)}, u32[]{:S(2)}) collective-permute-start(f32[32,64,128]{2,1,0:T(8,128)S(1)} %get-tuple-element.60), channel_id=1, source_target_pairs={{32,0},{64,32},{96,64},{33,1},{65,33},{97,65},{34,2},{66,34},{98,6... | collective-permute-start | bytes 3145736 | tf_op jit(solution)/shard_map/ppermute | solution.py:193
  65.7 7.1 %collective-permute-start.12 = (f32[4,64,1,128]{3,2,1,0:T(1,128)S(1)}, f32[4,64,1,128]{3,2,1,0:T(1,128)S(1)}, u32[]{:S(2)}, u32[]{:S(2)}) collective-permute-start(f32[4,64,1,128]{3,2,1,0:T(1,128)S(1)} %get-tuple-element.64), channel_id=1, source_target_pairs={{1,0},{2,1},{3,2},{5,4},{6,5},{7,6},{9,8},{10,9},{11,10},{13,12},{... | collective-permute-start | bytes 393224 | tf_op jit(solution)/shard_map/ppermute | solution.py:197
  72.8 10.5 %collective-permute-start.15 = (f32[4,1,64,128]{3,2,1,0:T(8,128)S(1)}, f32[4,1,64,128]{3,2,1,0:T(8,128)S(1)}, u32[]{:S(2)}, u32[]{:S(2)}) collective-permute-start(f32[4,1,64,128]{3,2,1,0:T(8,128)S(1)} %get-tuple-element.67), channel_id=1, source_target_pairs={{0,4},{4,8},{8,12},{12,16},{16,20},{20,24},{24,28},{1,5},{5,9},{9,... | collective-permute-start | bytes 393224 | tf_op jit(solution)/shard_map/ppermute | solution.py:196
  83.2 10.0 %collective-permute-start.10 = (f32[4,1,64,128]{3,2,1,0:T(8,128)S(1)}, f32[4,1,64,128]{3,2,1,0:T(8,128)S(1)}, u32[]{:S(2)}, u32[]{:S(2)}) collective-permute-start(f32[4,1,64,128]{3,2,1,0:T(8,128)S(1)} %get-tuple-element.62), channel_id=1, source_target_pairs={{4,0},{8,4},{12,8},{16,12},{20,16},{24,20},{28,24},{5,1},{9,5},{13... | collective-permute-start | bytes 393224 | tf_op jit(solution)/shard_map/ppermute | solution.py:196
  87.4 42.7 %collective-permute-start.21 = (f32[32,64,128]{2,1,0:T(8,128)S(1)}, f32[32,64,128]{2,1,0:T(8,128)S(1)}, u32[]{:S(2)}, u32[]{:S(2)}) collective-permute-start(f32[32,64,128]{2,1,0:T(8,128)S(1)} %get-tuple-element.77), channel_id=1, source_target_pairs={{0,32},{32,64},{64,96},{1,33},{33,65},{65,97},{2,34},{34,66},{66,9... | collective-permute-start | bytes 3145736 | tf_op jit(solution)/shard_map/ppermute | solution.py:193
  89.4 40.7 %collective-permute-start.22 = (f32[32,64,128]{2,1,0:T(8,128)S(1)}, f32[32,64,128]{2,1,0:T(8,128)S(1)}, u32[]{:S(2)}, u32[]{:S(2)}) collective-permute-start(f32[32,64,128]{2,1,0:T(8,128)S(1)} %get-tuple-element.78), channel_id=1, source_target_pairs={{32,0},{64,32},{96,64},{33,1},{65,33},{97,65},{34,2},{66,34},{98,6... | collective-permute-start | bytes 3145736 | tf_op jit(solution)/shard_map/ppermute | solution.py:193
  102.5 39.5 %collective-permute-start.16 = (f32[32,64,128]{2,1,0:T(8,128)S(1)}, f32[32,64,128]{2,1,0:T(8,128)S(1)}, u32[]{:S(2)}, u32[]{:S(2)}) collective-permute-start(f32[32,64,128]{2,1,0:T(8,128)S(1)} %get-tuple-element.71), channel_id=1, source_target_pairs={{0,32},{32,64},{64,96},{1,33},{33,65},{65,97},{2,34},{34,66},{66,9... | collective-permute-start | bytes 3145736 | tf_op jit(solution)/shard_map/ppermute | solution.py:193
  104.4 40.8 %collective-permute-start.17 = (f32[32,64,128]{2,1,0:T(8,128)S(1)}, f32[32,64,128]{2,1,0:T(8,128)S(1)}, u32[]{:S(2)}, u32[]{:S(2)}) collective-permute-start(f32[32,64,128]{2,1,0:T(8,128)S(1)} %get-tuple-element.72), channel_id=1, source_target_pairs={{32,0},{64,32},{96,64},{33,1},{65,33},{97,65},{34,2},{66,34},{98,6... | collective-permute-start | bytes 3145736 | tf_op jit(solution)/shard_map/ppermute | solution.py:193
  117.7 10.5 %collective-permute-start.23 = (f32[4,1,64,128]{3,2,1,0:T(8,128)S(1)}, f32[4,1,64,128]{3,2,1,0:T(8,128)S(1)}, u32[]{:S(2)}, u32[]{:S(2)}) collective-permute-start(f32[4,1,64,128]{3,2,1,0:T(8,128)S(1)} %get-tuple-element.79), channel_id=1, source_target_pairs={{0,4},{4,8},{8,12},{12,16},{16,20},{20,24},{24,28},{1,5},{5,9},{9,... | collective-permute-start | bytes 393224 | tf_op jit(solution)/shard_map/ppermute | solution.py:196
  147.4 12.8 %collective-permute-start.27 = (f32[4,64,1,128]{3,2,1,0:T(1,128)S(1)}, f32[4,64,1,128]{3,2,1,0:T(1,128)S(1)}, u32[]{:S(2)}, u32[]{:S(2)}) collective-permute-start(f32[4,64,1,128]{3,2,1,0:T(1,128)S(1)} %get-tuple-element.87), channel_id=1, source_target_pairs={{0,1},{1,2},{2,3},{4,5},{5,6},{6,7},{8,9},{9,10},{10,11},{12,13},{... | collective-permute-start | bytes 393224 | tf_op jit(solution)/shard_map/ppermute | solution.py:197
  149.4 10.8 %collective-permute-start.28 = (f32[4,64,1,128]{3,2,1,0:T(1,128)S(1)}, f32[4,64,1,128]{3,2,1,0:T(1,128)S(1)}, u32[]{:S(2)}, u32[]{:S(2)}) collective-permute-start(f32[4,64,1,128]{3,2,1,0:T(1,128)S(1)} %get-tuple-element.88), channel_id=1, source_target_pairs={{1,0},{2,1},{3,2},{5,4},{6,5},{7,6},{9,8},{10,9},{11,10},{13,12},{... | collective-permute-start | bytes 393224 | tf_op jit(solution)/shard_map/ppermute | solution.py:197
  150.7 10.9 %collective-permute-start.31 = (f32[4,1,64,128]{3,2,1,0:T(8,128)S(1)}, f32[4,1,64,128]{3,2,1,0:T(8,128)S(1)}, u32[]{:S(2)}, u32[]{:S(2)}) collective-permute-start(f32[4,1,64,128]{3,2,1,0:T(8,128)S(1)} %get-tuple-element.91), channel_id=1, source_target_pairs={{0,4},{4,8},{8,12},{12,16},{16,20},{20,24},{24,28},{1,5},{5,9},{9,... | collective-permute-start | bytes 393224 | tf_op jit(solution)/shard_map/ppermute | solution.py:196
  153.9 18.6 %collective-permute-start.26 = (f32[4,1,64,128]{3,2,1,0:T(8,128)S(1)}, f32[4,1,64,128]{3,2,1,0:T(8,128)S(1)}, u32[]{:S(2)}, u32[]{:S(2)}) collective-permute-start(f32[4,1,64,128]{3,2,1,0:T(8,128)S(1)} %get-tuple-element.86), channel_id=1, source_target_pairs={{4,0},{8,4},{12,8},{16,12},{20,16},{24,20},{28,24},{5,1},{9,5},{13... | collective-permute-start | bytes 393224 | tf_op jit(solution)/shard_map/ppermute | solution.py:196
  164.0 27.9 %collective-permute-start.35 = (f32[32,64,128]{2,1,0:T(8,128)S(1)}, f32[32,64,128]{2,1,0:T(8,128)S(1)}, u32[]{:S(2)}, u32[]{:S(2)}) collective-permute-start(f32[32,64,128]{2,1,0:T(8,128)S(1)} %shard_map.50.total), channel_id=1, source_target_pairs={{0,32},{32,64},{1,33},{33,65},{2,34},{34,66},{3,35},{35,67},{4,36}... | collective-permute-start | bytes 3145736 | tf_op jit(solution)/shard_map/ppermute | solution.py:253
  165.3 28.5 %collective-permute-start.36 = (f32[32,64,128]{2,1,0:T(8,128)S(1)}, f32[32,64,128]{2,1,0:T(8,128)S(1)}, u32[]{:S(2)}, u32[]{:S(2)}) collective-permute-start(f32[32,64,128]{2,1,0:T(8,128)S(1)} %shard_map.50.total), channel_id=1, source_target_pairs={{0,96},{1,97},{2,98},{3,99},{4,100},{5,101},{6,102},{7,103},{8,104... | collective-permute-start | bytes 3145736 | tf_op jit(solution)/shard_map/ppermute | solution.py:254
  166.0 48.4 %collective-permute-start.29 = (f32[32,64,128]{2,1,0:T(8,128)S(1)}, f32[32,64,128]{2,1,0:T(8,128)S(1)}, u32[]{:S(2)}, u32[]{:S(2)}) collective-permute-start(f32[32,64,128]{2,1,0:T(8,128)S(1)} %get-tuple-element.89), channel_id=1, source_target_pairs={{0,32},{32,64},{64,96},{1,33},{33,65},{65,97},{2,34},{34,66},{66,9... | collective-permute-start | bytes 3145736 | tf_op jit(solution)/shard_map/ppermute | solution.py:193
  168.0 48.4 %collective-permute-start.30 = (f32[32,64,128]{2,1,0:T(8,128)S(1)}, f32[32,64,128]{2,1,0:T(8,128)S(1)}, u32[]{:S(2)}, u32[]{:S(2)}) collective-permute-start(f32[32,64,128]{2,1,0:T(8,128)S(1)} %get-tuple-element.90), channel_id=1, source_target_pairs={{32,0},{64,32},{96,64},{33,1},{65,33},{97,65},{34,2},{66,34},{98,6... | collective-permute-start | bytes 3145736 | tf_op jit(solution)/shard_map/ppermute | solution.py:193
  174.9 45.4 %collective-permute-start.33 = (f32[32,64,128]{2,1,0:T(8,128)S(1)}, f32[32,64,128]{2,1,0:T(8,128)S(1)}, u32[]{:S(2)}, u32[]{:S(2)}) collective-permute-start(f32[32,64,128]{2,1,0:T(8,128)S(1)} %shard_map.49), channel_id=1, source_target_pairs={{0,96},{32,0},{1,97},{33,1},{2,98},{34,2},{3,99},{35,3},{4,100},{3... | collective-permute-start | bytes 3145736 | tf_op jit(solution)/shard_map/ppermute | solution.py:255
  191.9 44.9 %collective-permute-start.24 = (f32[32,64,128]{2,1,0:T(8,128)S(1)}, f32[32,64,128]{2,1,0:T(8,128)S(1)}, u32[]{:S(2)}, u32[]{:S(2)}) collective-permute-start(f32[32,64,128]{2,1,0:T(8,128)S(1)} %get-tuple-element.83), channel_id=1, source_target_pairs={{0,32},{32,64},{64,96},{1,33},{33,65},{65,97},{2,34},{34,66},{66,9... | collective-permute-start | bytes 3145736 | tf_op jit(solution)/shard_map/ppermute | solution.py:193
  193.9 43.0 %collective-permute-start.25 = (f32[32,64,128]{2,1,0:T(8,128)S(1)}, f32[32,64,128]{2,1,0:T(8,128)S(1)}, u32[]{:S(2)}, u32[]{:S(2)}) collective-permute-start(f32[32,64,128]{2,1,0:T(8,128)S(1)} %get-tuple-element.84), channel_id=1, source_target_pairs={{32,0},{64,32},{96,64},{33,1},{65,33},{97,65},{34,2},{66,34},{98,6... | collective-permute-start | bytes 3145736 | tf_op jit(solution)/shard_map/ppermute | solution.py:193
  214.4 29.9 %collective-permute-start.37 = (f32[32,64,128]{2,1,0:T(8,128)S(1)}, f32[32,64,128]{2,1,0:T(8,128)S(1)}, u32[]{:S(2)}, u32[]{:S(2)}) collective-permute-start(f32[32,64,128]{2,1,0:T(8,128)S(1)} %shard_map.51), channel_id=1, source_target_pairs={{64,96},{96,64},{65,97},{97,65},{66,98},{98,66},{67,99},{99,67},{6... | collective-permute-start | bytes 3145736 | tf_op jit(solution)/shard_map/ppermute | solution.py:257
  216.3 45.0 %collective-permute-start.32 = (f32[32,64,128]{2,1,0:T(8,128)S(1)}, f32[32,64,128]{2,1,0:T(8,128)S(1)}, u32[]{:S(2)}, u32[]{:S(2)}) collective-permute-start(f32[32,64,128]{2,1,0:T(8,128)S(1)} %shard_map.49), channel_id=1, source_target_pairs={{0,32},{32,64},{64,96},{1,33},{33,65},{65,97},{2,34},{34,66},{66,9... | collective-permute-start | bytes 3145736 | tf_op jit(solution)/shard_map/ppermute | solution.py:258
  220.3 45.2 %collective-permute-start.34 = (f32[32,64,128]{2,1,0:T(8,128)S(1)}, f32[32,64,128]{2,1,0:T(8,128)S(1)}, u32[]{:S(2)}, u32[]{:S(2)}) collective-permute-start(f32[32,64,128]{2,1,0:T(8,128)S(1)} %collective-permute-done.33.two), channel_id=1, source_target_pairs={{96,64},{0,96},{97,65},{1,97},{98,66},{2,98},{99,67},{3,99},{100,6... | collective-permute-start | bytes 3145736 | tf_op jit(solution)/shard_map/ppermute | solution.py:259
  (8 other events, 67.6 us)
